TPU v7x, 8 devices: a whole 2x2x1 slice. The times are simulated.
8 devices in a mesh: f: 4 (over z, y, x), h: 2 (over core).
Axes of the slice: x: 2, y: 2, z: 1, core: 2. Of those that a mesh axis runs over, the one named last changes fastest.
Arguments:
- x: bfloat16 [64, 5120], P(None, 'h')
- g1: float32 [5120], P('h')
- g2: float32 [5120], P('h')
- w_gate: bfloat16 [5120, 13824], P('h', 'f')
- w_up: bfloat16 [5120, 13824], P('h', 'f')
- w_down: bfloat16 [13824, 5120], P('f', 'h')
- o: bfloat16 [64, 5120], P(None, 'f')
- w_o: bfloat16 [5120, 5120], P('f', 'h')
- w_qkv: bfloat16 [5120, 15360], P('h', 'f')
Outputs:
- output 1: bfloat16 [64, 5120], P(None, 'h')
- output 2: bfloat16 [64, 15360], P(None, 'f')
All inputs are finite; a program needn't handle non-finite values.
Results may differ from a plain program's by a relative error of at most 0.00390993.
Values are sent between devices in bfloat16 or wider.
A program may use at most 1 GiB of HBM per device.

v0:
```python
import jax
import jax.numpy as jnp
from jax import lax
from jax.sharding import PartitionSpec as P

EPS = 1e-6


def _dot(a, b):
    return jnp.dot(a, b, preferred_element_type=jnp.float32)


def _norm(x, g, d):
    xf = x.astype(jnp.float32)
    ss = lax.psum(jnp.sum(xf * xf, axis=-1, keepdims=True), 'h')
    r = lax.rsqrt(ss / d + EPS)
    return (xf * r * g).astype(jnp.bfloat16)


def solution(mesh):
    h = mesh.shape['h']

    def body(x, g1, g2, w_gate, w_up, w_down, o, w_o, w_qkv):
        d = x.shape[1] * h
        n = _norm(x, g1, d)
        gt, up = lax.psum((_dot(n, w_gate), _dot(n, w_up)), 'h')
        a = (jax.nn.silu(gt) * up).astype(jnp.bfloat16)
        y = lax.psum(_dot(a, w_down) + _dot(o, w_o), 'f')
        x_next = (x.astype(jnp.float32) + y).astype(jnp.bfloat16)
        n1 = _norm(x_next, g2, d)
        qkv = lax.psum(_dot(n1, w_qkv), 'h').astype(jnp.bfloat16)
        return x_next, qkv

    in_specs = (P(None, 'h'), P('h'), P('h'), P('h', 'f'), P('h', 'f'), P('f', 'h'),
                P(None, 'f'), P('f', 'h'), P('h', 'f'))
    return jax.shard_map(body, mesh=mesh, in_specs=in_specs,
                         out_specs=(P(None, 'h'), P(None, 'f')), check_vma=False)
```

profile of v0, /device:TPU:0, one launch (start us, length us, event | category | flops | bytes accessed | tf_op | source)
XLA Modules:
  0.0 120.0 jit_solution(5627529914823916213)
XLA Ops:
  7.2 0.0 copy-start
  7.2 0.0 copy-start.2
  7.2 0.0 copy-start.4
  7.2 0.0 all-reduce.7.cloned.1.call-start
  7.2 1.2 fusion.3
  8.5 3.0 %psum.42 = f32[64,1]{0,1:T(1,128)S(1)} all-reduce(f32[64,1]{0,1:T(1,128)S(1)} %bitcast.15), channel_id=1, replica_groups=mesh['f'=4,'h'=2] {'h'}, use_global_device_ids=true, to_apply=%region_1.0 | all-reduce | flops 64 | bytes 512 | tf_op jit(solution)/shard_map/psum | solution.py:15
  11.4 0.0 copy-start.1
  11.5 10.5 %fusion.13 = f32[64,3456]{1,0:T(8,128)} fusion(bf16[2560,3456]{1,0:T(8,128)(2,1)} %param.13, bf16[64,2560]{1,0:T(8,128)(2,1)} %param.9, f32[2560]{0:T(1024)} %param.10, f32[64]{0:T(128)S(1)} %rsqrt_bitcast_fusion.1), kind=kOutput, calls=%fused_computation.19 | convolution fusion | flops 1133117440 | bytes 18917632 | tf_op jit(solution)/shard_map/dot_general | solution.py:10
  21.9 0.0 copy-done.2
  21.9 0.0 copy-done.4
  21.9 1.0 copy-done.1
  22.9 4.2 %fusion.15 = f32[64,3456]{1,0:T(8,128)} fusion(bf16[2560,3456]{1,0:T(8,128)(2,1)S(1)} %copy-done.1, bf16[64,2560]{1,0:T(8,128)(2,1)S(1)} %copy-done.2, f32[2560]{0:T(1024)S(1)} %copy-done.4, f32[64]{0:T(128)S(1)} %rsqrt_bitcast_fusion.1), kind=kOutput, calls=%fused_computation.20 | convolution fusion | flops 1133117440 | bytes 18917632 | tf_op jit(solution)/shard_map/dot_general | solution.py:10
  27.1 0.0 slice-start
  27.1 0.0 all-reduce.7.cloned.1.call-update
  27.2 0.0 all-reduce.5.cloned.1.call-start
  27.2 16.9 %all-reduce.7.cloned.1.call-done = (f32[64,3456]{1,0:T(8,128)}, f32[64,3456]{1,0:T(8,128)}) async-done(((f32[64,3456]{1,0:T(8,128)}, f32[64,3456]{1,0:T(8,128)}), (f32[64,3456]{1,0:T(8,128)}, f32[64,3456]{1,0:T(8,128)})) %all-reduce.7.cloned.1.call-update) | async-done | bytes 1769488 | tf_op jit(solution)/shard_map/psum | solution.py:26
  44.1 0.0 slice-start.1
  44.1 0.0 copy-start.5
  44.1 9.9 %fusion.7 = f32[64,2560]{1,0:T(8,128)S(1)} fusion(bf16[3456,2560]{1,0:T(8,128)(2,1)} %param.14, f32[64,3456]{1,0:T(8,128)} %get-tuple-element.2, f32[64,3456]{1,0:T(8,128)} %get-tuple-element.3), kind=kOutput, calls=%fused_computation.14 | convolution fusion | flops 1133789184 | bytes 20119552 | tf_op jit(solution)/shard_map/dot_general | solution.py:10
  54.0 0.0 copy-done
  54.0 0.0 slice-done
  54.0 0.0 slice-done.1
  54.0 2.1 %convolution_add_fusion = f32[64,2560]{1,0:T(8,128)} fusion(f32[64,2560]{1,0:T(8,128)S(1)} %fusion.7, bf16[64,1280]{1,0:T(8,128)(2,1)S(1)} %copy-done, bf16[1280,2560]{1,0:T(8,128)(2,1)S(1)} %bitcast.13), kind=kOutput, calls=%fused_computation | convolution fusion | flops 419594240 | bytes 8028160 | tf_op jit(solution)/shard_map/dot_general | solution.py:10
  56.1 0.0 all-reduce.5.cloned.1.call-update
  56.2 36.5 %all-reduce.5.cloned.1.call-done = f32[64,2560]{1,0:T(8,128)} async-done(((f32[64,2560]{1,0:T(8,128)}), f32[64,2560]{1,0:T(8,128)}) %all-reduce.5.cloned.1.call-update) | async-done | bytes 655376 | tf_op jit(solution)/shard_map/psum | solution.py:28
  92.7 1.3 %fusion = (f32[64]{0:T(128)S(1)}, bf16[64,2560]{1,0:T(8,128)(2,1)S(1)}) fusion(f32[64,2560]{1,0:T(8,128)} %all-reduce.5.cloned.1.call-done, bf16[64,2560]{1,0:T(8,128)(2,1)S(1)} %copy-done.2), kind=kLoop, calls=%fused_computation.7 | loop fusion | flops 982976 | bytes 1310976 | tf_op jit(solution)/shard_map/reduce_sum | solution.py:15
  94.0 0.0 copy-start.3
  94.0 2.5 %psum.46 = f32[64,1]{0,1:T(1,128)S(1)} all-reduce(f32[64,1]{0,1:T(1,128)S(1)} %bitcast.14), channel_id=1, replica_groups=mesh['f'=4,'h'=2] {'h'}, use_global_device_ids=true, to_apply=%region_6.7 | all-reduce | flops 64 | bytes 512 | tf_op jit(solution)/shard_map/psum | solution.py:15
  96.5 0.0 copy-done.5
  96.5 10.2 %fusion.9 = f32[64,3840]{1,0:T(8,128)S(1)} fusion(bf16[2560,3840]{1,0:T(8,128)(2,1)} %param.17, bf16[64,2560]{1,0:T(8,128)(2,1)S(1)} %get-tuple-element.5, f32[2560]{0:T(1024)S(1)} %copy-done.5, f32[64]{0:T(128)S(1)} %rsqrt_bitcast_fusion), kind=kOutput, calls=%fused_computation.16 | convolution fusion | flops 1258946560 | bytes 20982016 | tf_op jit(solution)/shard_map/dot_general | solution.py:10
  106.7 6.5 %all-reduce.8 = bf16[64,3840]{1,0:T(8,128)(2,1)} all-reduce(f32[64,3840]{1,0:T(8,128)S(1)} %fusion.9), channel_id=1, replica_groups=mesh['f'=4,'h'=2] {'h'}, use_global_device_ids=true, to_apply=%region_7.8 | all-reduce | flops 245760 | bytes 1474560 | tf_op jit(solution)/shard_map/psum | solution.py:31
  113.2 0.0 copy-done.3
  (3 shorter events, 0.0 us)
Async XLA Ops:
  7.2 46.8 %copy-start = (bf16[64,1280]{1,0:T(8,128)(2,1)S(1)}, bf16[64,1280]{1,0:T(8,128)(2,1)}, u32[]{:S(2)}) copy-start(bf16[64,1280]{1,0:T(8,128)(2,1)} %param.15) | copy-start | bytes 491524
  7.2 14.7 %copy-start.2 = (bf16[64,2560]{1,0:T(8,128)(2,1)S(1)}, bf16[64,2560]{1,0:T(8,128)(2,1)}, u32[]{:S(2)}) copy-start(bf16[64,2560]{1,0:T(8,128)(2,1)} %param.9) | copy-start | bytes 983044
  7.2 14.7 %copy-start.4 = (f32[2560]{0:T(1024)S(1)}, f32[2560]{0:T(1024)}, u32[]{:S(2)}) copy-start(f32[2560]{0:T(1024)} %param.10) | copy-start | bytes 30724
  7.2 36.9 %all-reduce.7.cloned.1.call-start = ((), (), s32[]{:S(2)}) async-start(), calls=%async_computation.1 | async-start | bytes 3538944 | tf_op jit(solution)/shard_map/psum | solution.py:26
  11.4 11.5 %copy-start.1 = (bf16[2560,3456]{1,0:T(8,128)(2,1)S(1)}, bf16[2560,3456]{1,0:T(8,128)(2,1)}, u32[]{:S(2)}) copy-start(bf16[2560,3456]{1,0:T(8,128)(2,1)} %param.12) | copy-start | bytes 53084164
  27.1 26.9 %slice-start = ((s8[6553600]{0:T(1024)(128)(4,1)}), s8[2359296]{0:T(1024)(128)(4,1)S(1)}, s32[]{:S(2)}) async-start(s8[6553600]{0:T(1024)(128)(4,1)} %bitcast.12), calls=%async_computation.2 | async-start | bytes 4718592
  27.2 65.5 %all-reduce.5.cloned.1.call-start = ((), (), s32[]{:S(2)}) async-start(), calls=%async_computation | async-start | bytes 1310720 | tf_op jit(solution)/shard_map/psum | solution.py:28
  44.1 9.9 %slice-start.1 = ((s8[6553600]{0:T(1024)(128)(4,1)}), s8[4194304]{0:T(1024)(128)(4,1)S(1)}, s32[]{:S(2)}) async-start(s8[6553600]{0:T(1024)(128)(4,1)} %bitcast.12), calls=%async_computation.3 | async-start | bytes 8388608
  44.1 52.3 %copy-start.5 = (f32[2560]{0:T(1024)S(1)}, f32[2560]{0:T(1024)}, u32[]{:S(2)}) copy-start(f32[2560]{0:T(1024)} %param.11) | copy-start | bytes 30724
  94.0 19.2 %copy-start.3 = (bf16[64,2560]{1,0:T(8,128)(2,1)}, bf16[64,2560]{1,0:T(8,128)(2,1)S(1)}, u32[]{:S(2)}) copy-start(bf16[64,2560]{1,0:T(8,128)(2,1)S(1)} %get-tuple-element.5) | copy-start | bytes 983044
Sparse Core Ops, SparseCore 0:
  27.3 16.7 all-reduce.6
  56.3 36.3 all-reduce.4
where the time goes:
time: 120 us
  waiting for transfers between devices  53.5 us (45%)
  matrix products  36.8 us (31%)
  between operations  14.1 us (12%)
  blocking collectives  12 us (10%)
  other arithmetic  2.5 us (2%)
    dot_general x5, matrix products, _dot(): return jnp.dot(a, b, preferred_element_type=jnp.float32)  36.8 us
    psum x1, waiting for transfers between devices, body(): y = lax.psum(_dot(a, w_down) + _dot(o, w_o), 'f')  36.5 us
    psum x1, waiting for transfers between devices, body(): gt, up = lax.psum((_dot(n, w_gate), _dot(n, w_up)), 'h')  16.9 us
    psum x1, blocking collectives, body(): qkv = lax.psum(_dot(n1, w_qkv), 'h').astype(jnp.bfloat16)  6.51 us
    psum x2, blocking collectives, _norm(): ss = lax.psum(jnp.sum(xf * xf, axis=-1, keepdims=True), 'h')  5.46 us
    reduce_sum x2, other arithmetic, _norm(): ss = lax.psum(jnp.sum(xf * xf, axis=-1, keepdims=True), 'h')  2.48 us
  transfers between devices with their start and end apart: 2, of which 2 were waited for; matrix products, arithmetic and copies ran while one was open for 0% of the time, Pallas kernels for 0%

commit v1 on v0

v1 whole, which is shorter than its diff:
```python
import functools

import jax
import jax.numpy as jnp
from jax import lax
from jax.experimental import pallas as pl
from jax.experimental.pallas import tpu as pltpu
from jax.sharding import PartitionSpec as P

EPS = 1e-6
MESH = pl.DeviceIdType.MESH
F32, BF16 = jnp.float32, jnp.bfloat16


def _dot(a, b):
    return jnp.dot(a, b, preferred_element_type=F32)


def _kernel(cfg, x_hbm, g1_hbm, g2_hbm, wg_hbm, wu_hbm, wd_hbm, o_hbm, wo_hbm, wq_hbm,
            xo_hbm, qo_hbm,
            ring, wdv, xv, gv, oa, nv, xnv, ss1, ss2, pown, prec, ysend, yrec, qown, qrec, qout,
            s_in, s_wg, s_wu, s_wd, s_wo, s_wq, s_out,
            c_ss, c_p, c_y_s, c_y_r, c_x_s, c_x_r, c_s2_s, c_s2_r, c_q):
    d, kd, ko, slots, half, ng, cw, ny, qw, nq, rows = cfg
    f, h = lax.axis_index('f'), lax.axis_index('h')
    partner = (f, 1 - h)
    fx = [f, f + 1 - 2 * lax.rem(f, 2), lax.rem(f + 2, 4), 3 - f]

    def small():
        return [pltpu.make_async_copy(x_hbm, xv, s_in.at[0]),
                pltpu.make_async_copy(g1_hbm, gv.at[pl.ds(0, 1)], s_in.at[1]),
                pltpu.make_async_copy(g2_hbm, gv.at[pl.ds(1, 1)], s_in.at[2]),
                pltpu.make_async_copy(o_hbm, oa.at[:, pl.ds(0, ko)], s_in.at[3])]

    def gu(j):
        slot, cols = lax.rem(j, slots), pl.ds(pl.multiple_of(j * half, 128), half)
        return [pltpu.make_async_copy(wg_hbm.at[:, cols], ring.at[slot, :, pl.ds(0, half)], s_wg.at[j]),
                pltpu.make_async_copy(wu_hbm.at[:, cols], ring.at[slot, :, pl.ds(half, half)], s_wu.at[j])]

    def dn(c):
        cols = pl.ds(pl.multiple_of(c * cw, 128), cw)
        return [pltpu.make_async_copy(wo_hbm.at[:, cols], wdv.at[c, pl.ds(0, ko)], s_wo.at[c]),
                pltpu.make_async_copy(wd_hbm.at[:, cols], wdv.at[c, pl.ds(ko, kd)], s_wd.at[c])]

    def qk(j):
        slot, cols = lax.rem(j + ng, slots), pl.ds(pl.multiple_of(j * qw, 128), qw)
        return [pltpu.make_async_copy(wq_hbm.at[:, cols], ring.at[slot], s_wq.at[j])]

    def start(copies):
        for c in copies:
            c.start()

    def wait(copies):
        for c in copies:
            c.wait()

    ins = small()
    start(ins)
    for j in range(slots):
        start(gu(j))

    barrier = pltpu.get_barrier_semaphore()
    for k in range(4):
        for t in range(2):
            if k or t:
                pl.semaphore_signal(barrier, inc=1, device_id=(fx[k], h if t == 0 else 1 - h), device_id_type=MESH)

    wait(ins)
    xf = xv[...].astype(F32)
    s = jnp.sum(xf * xf, axis=-1, keepdims=True)
    ss1[h] = jnp.broadcast_to(s, ss1.shape[1:])
    pl.semaphore_wait(barrier, 7)
    ex = pltpu.make_async_remote_copy(ss1.at[h], ss1.at[h], c_ss.at[0], c_ss.at[1], partner, MESH)
    ex.start()
    ex.wait()
    r = lax.rsqrt((ss1[0] + ss1[1])[:, :1] / (2 * d) + EPS)
    nv[...] = (xv[...].astype(F32) * r * gv[0:1, :]).astype(BF16)

    def pcopy(j):
        return pltpu.make_async_remote_copy(pown.at[j], prec.at[j], c_p.at[0, j], c_p.at[1, j], partner, MESH)

    def act(j):
        pcopy(j).wait_recv()
        g = pown[j, :, :half] + prec[j, :, :half]
        u = pown[j, :, half:] + prec[j, :, half:]
        oa[:, pl.ds(pl.multiple_of(ko + j * half, 128), half)] = (g / (1.0 + jnp.exp(-g)) * u).astype(BF16)

    def gu_step(j, _):
        wait(gu(j))
        pown[j] = _dot(nv[...], ring[lax.rem(j, slots)])
        pcopy(j).start()

        @pl.when(j + slots < ng)
        def _():
            start(gu(j + slots))

        @pl.when(j + slots == ng - 1)
        def _():
            for c in range(ny):
                start(dn(c))

        @pl.when((j + slots >= ng) & (j + slots < ng + nq))
        def _():
            start(qk(j + slots - ng))

        @pl.when(j > 0)
        def _():
            act(j - 1)
        return 0

    lax.fori_loop(0, ng, gu_step, 0)
    act(ng - 1)

    def ycopy(c, k):
        blk = pl.ds(pl.multiple_of(fx[k] * rows, rows), rows)
        return pltpu.make_async_remote_copy(ysend.at[c, blk], yrec.at[k - 1, c], c_y_s.at[k - 1, c], c_y_r.at[k - 1, c],
                                            (fx[k], h), MESH)

    def dn_step(c, _):
        wait(dn(c))
        ysend[c] = _dot(oa[...], wdv[c])
        for k in (3, 1, 2):
            ycopy(c, k).start()
        return 0

    lax.fori_loop(0, ny, dn_step, 0)

    mine = pl.ds(pl.multiple_of(f * rows, rows), rows)

    def xcopy(c, k):
        cols = pl.ds(c * cw, cw)
        return pltpu.make_async_remote_copy(xnv.at[mine, cols], xnv.at[mine, cols], c_x_s.at[k - 1, c], c_x_r.at[k - 1, c],
                                            (fx[k], h), MESH)

    s = jnp.zeros((rows, 1), F32)
    for c in range(ny):
        for k in (1, 2, 3):
            ycopy(c, k).wait_recv()
        y = (ysend[c, mine] + yrec[0, c]) + (yrec[1, c] + yrec[2, c])
        xn = (xv[mine, c * cw:(c + 1) * cw].astype(F32) + y).astype(BF16)
        xnv[mine, c * cw:(c + 1) * cw] = xn
        xf = xn.astype(F32)
        s = s + jnp.sum(xf * xf, axis=-1, keepdims=True)
        if c < ny - 1:
            for k in (3, 1, 2):
                xcopy(c, k).start()
    ss2[h, mine] = jnp.broadcast_to(s, (rows, 128))

    def scopy(k, t):
        i = k * 2 + t - 1
        return pltpu.make_async_remote_copy(ss2.at[h, mine], ss2.at[h, mine], c_s2_s.at[i], c_s2_r.at[i],
                                            (fx[k], h if t == 0 else 1 - h), MESH)

    peers = [(k, t) for k in (3, 1, 2, 0) for t in (0, 1) if k or t]
    for k, t in peers:
        scopy(k, t).start()
    for k in (3, 1, 2):
        xcopy(ny - 1, k).start()
    for k, t in peers:
        scopy(k, t).wait_recv()
    r = lax.rsqrt((ss2[0] + ss2[1])[:, :1] / (2 * d) + EPS)
    for c in range(ny):
        for k in (1, 2, 3):
            xcopy(c, k).wait_recv()
        cols = slice(c * cw, (c + 1) * cw)
        nv[:, cols] = (xnv[:, cols].astype(F32) * r * gv[1:2, cols]).astype(BF16)
    xout = pltpu.make_async_copy(xnv, xo_hbm, s_out.at[nq])
    xout.start()

    def qcopy(j):
        return pltpu.make_async_remote_copy(qown.at[j], qrec.at[j], c_q.at[0, j], c_q.at[1, j], partner, MESH)

    def oput(j):
        cols = pl.ds(pl.multiple_of(j * qw, 128), qw)
        return pltpu.make_async_copy(qout.at[:, cols], qo_hbm.at[:, cols], s_out.at[j])

    def fin(j):
        qcopy(j).wait_recv()
        qout[:, pl.ds(pl.multiple_of(j * qw, 128), qw)] = (qown[j] + qrec[j]).astype(BF16)
        oput(j).start()

    def q_step(j, _):
        wait(qk(j))
        qown[j] = _dot(nv[...], ring[lax.rem(j + ng, slots)])
        qcopy(j).start()

        @pl.when(j > 0)
        def _():
            fin(j - 1)
        return 0

    lax.fori_loop(0, nq, q_step, 0)
    fin(nq - 1)

    for j in range(ng):
        pcopy(j).wait_send()
    for c in range(ny):
        for k in (1, 2, 3):
            ycopy(c, k).wait_send()
            xcopy(c, k).wait_send()
    for k, t in peers:
        scopy(k, t).wait_send()
    for j in range(nq):
        qcopy(j).wait_send()
        oput(j).wait()
    xout.wait()


def solution(mesh):
    def body(x, g1, g2, w_gate, w_up, w_down, o, w_o, w_qkv):
        t, d = x.shape
        kd, ko, q = w_down.shape[0], w_o.shape[0], w_qkv.shape[1]
        slots, half, cw, qw = 6, 384, 512, 768
        ng, ny, nq, rows = kd // half, d // cw, q // qw, t // 4
        cfg = (d, kd, ko, slots, half, ng, cw, ny, qw, nq, rows)
        dma = pltpu.SemaphoreType.DMA
        any_ = pl.BlockSpec(memory_space=pl.ANY)
        return pl.pallas_call(
            functools.partial(_kernel, cfg),
            out_shape=(jax.ShapeDtypeStruct((t, d), BF16), jax.ShapeDtypeStruct((t, q), BF16)),
            in_specs=[any_] * 9,
            out_specs=(any_, any_),
            scratch_shapes=[
                pltpu.VMEM((slots, d, 2 * half), BF16),
                pltpu.VMEM((ny, ko + kd, cw), BF16),
                pltpu.VMEM((t, d), BF16),
                pltpu.VMEM((2, d), F32),
                pltpu.VMEM((t, ko + kd), BF16),
                pltpu.VMEM((t, d), BF16),
                pltpu.VMEM((t, d), BF16),
                pltpu.VMEM((2, t, 128), F32),
                pltpu.VMEM((2, t, 128), F32),
                pltpu.VMEM((ng, t, 2 * half), F32),
                pltpu.VMEM((ng, t, 2 * half), F32),
                pltpu.VMEM((ny, t, cw), F32),
                pltpu.VMEM((3, ny, rows, cw), F32),
                pltpu.VMEM((nq, t, qw), F32),
                pltpu.VMEM((nq, t, qw), F32),
                pltpu.VMEM((t, q), BF16),
                dma((4,)), dma((ng,)), dma((ng,)), dma((ny,)), dma((ny,)), dma((nq,)), dma((nq + 1,)),
                dma((2,)), dma((2, ng)), dma((3, ny)), dma((3, ny)), dma((3, ny)), dma((3, ny)),
                dma((7,)), dma((7,)), dma((2, nq)),
            ],
            compiler_params=pltpu.CompilerParams(collective_id=0, has_side_effects=True,
                                                 vmem_limit_bytes=66_000_000),
            name='block',
        )(x, g1.reshape(1, -1), g2.reshape(1, -1), w_gate, w_up, w_down, o, w_o, w_qkv)

    in_specs = (P(None, 'h'), P('h'), P('h'), P('h', 'f'), P('h', 'f'), P('f', 'h'),
                P(None, 'f'), P('f', 'h'), P('h', 'f'))
    return jax.shard_map(body, mesh=mesh, in_specs=in_specs,
                         out_specs=(P(None, 'h'), P(None, 'f')), check_vma=False)
```

time: 120 us -> 52.9 us (0.44)
  waiting for transfers between devices: 53.5 us -> 0 us
  Pallas kernels: 0 us -> 45.8 us
  matrix products: 36.8 us -> 0 us
  between operations: 14.1 us -> 0.64 us
  blocking collectives: 12 us -> 0 us
  local copies, waits for them, and re-layouts: 1.06 us -> 6.18 us
  other arithmetic: 2.5 us -> 0 us
    psum x2 -> x0, waiting for transfers between devices: 53.4 us -> none  [the longest x1 36.5 us: body(): y = lax.psum(_dot(a, w_down) + _dot(o, w_o), 'f')]
    pallas_call x0 -> x1, Pallas kernels: none -> 45.8 us  [body(): pl.pallas_call(functools.partial(_kernel, cfg), out_shape=(jax.ShapeDtype...]
    dot_general x5 -> x0, matrix products: 36.8 us -> none  [_dot(): return jnp.dot(a, b, preferred_element_type=jnp.float32)]
    psum x3 -> x0, blocking collectives: 12 us -> none  [the longest x1 6.51 us: body(): qkv = lax.psum(_dot(n1, w_qkv), 'h').astype(jnp.bfloat16)]
    reshape x0 -> x2, local copies, waits for them, and re-layouts: none -> 2.63 us  [the longest x1 1.31 us: body(): g1.reshape(1, -1)]
    unnamed x16 -> x2, local copies, waits for them, and re-layouts: 1.06 us -> 3.56 us
    reduce_sum x2 -> x0, other arithmetic: 2.48 us -> none  [_norm(): ss = lax.psum(jnp.sum(xf * xf, axis=-1, keepdims=True), 'h')]
  transfers between devices with their start and end apart: 2 -> 0, of which waited for: 2 -> 0; matrix products, arithmetic and copies ran while one was open for 0% -> 0% of each run, Pallas kernels for 0% -> 0%
where the time goes in v1:
time: 52.9 us; the launch traced here: 52.6 us
  Pallas kernels  45.8 us (87%)
  local copies, waits for them, and re-layouts  6.18 us (12%)
  between operations  0.64 us (1%)
    pallas_call x1, Pallas kernels, body(): pl.pallas_call(functools.partial(_kernel, cfg), out_shape=(jax.ShapeDtype...  45.8 us
    unnamed x2, local copies, waits for them, and re-layouts  3.56 us
    reshape x1, local copies, waits for them, and re-layouts, body(): g1.reshape(1, -1)  1.31 us
    reshape x1, local copies, waits for them, and re-layouts, body(): g2.reshape(1, -1)  1.31 us

profile of v1, /device:TPU:0, one launch (start us, length us, event | category | flops | bytes accessed | tf_op | source)
XLA Modules:
  0.0 52.6 jit_solution(17266150014625151907)
XLA Ops:
  0.6 1.3 %reshape.10.g1_hbm = f32[1,2560]{1,0:T(1,128)} reshape(f32[2560]{0:T(1024)} %param.10) | data formatting | bytes 20480 | tf_op jit(solution)/shard_map/reshape | solution.py:247
  1.9 1.3 %reshape.11.g2_hbm = f32[1,2560]{1,0:T(1,128)} reshape(f32[2560]{0:T(1024)} %param.11) | data formatting | bytes 20480 | tf_op jit(solution)/shard_map/reshape | solution.py:247
  3.3 45.8 %block.1 = (bf16[64,2560]{1,0:T(8,128)(2,1)}, bf16[64,3840]{1,0:T(8,128)(2,1)}) custom-call(bf16[64,2560]{1,0:T(8,128)(2,1)} %x_hbm.1, f32[1,2560]{1,0:T(1,128)} %reshape.10.g1_hbm, f32[1,2560]{1,0:T(1,128)} %reshape.11.g2_hbm, bf16[2560,3456]{1,0:T(8,128)(2,1)} %wg_hbm.1, bf16[2560,3456]{1,0:T(8,128)(2,1)} %wu_hbm.1, bf16[3456,2560]{1,0:T(8,128)(2,1)} %wd_hbm.1, ...), custom_call_target="tpu_custom_call" | custom-call | tf_op jit(solution)/shard_map/block/pallas_call | solution.py:218
  49.1 1.7 %copy.13 = bf16[64,2560]{1,0:T(8,128)(2,1)} copy(bf16[64,2560]{1,0:T(8,128)(2,1)} %get-tuple-element.4) | data formatting | bytes 655360
  50.8 1.8 %copy.14 = bf16[64,3840]{1,0:T(8,128)(2,1)} copy(bf16[64,3840]{1,0:T(8,128)(2,1)} %get-tuple-element.5) | data formatting | bytes 983040

commit v2 on v1

--- a/solution.py
+++ b/solution.py
@@ -17,9 +17,9 @@
 
 
 def _kernel(cfg, x_hbm, g1_hbm, g2_hbm, wg_hbm, wu_hbm, wd_hbm, o_hbm, wo_hbm, wq_hbm,
-            xo_hbm, qo_hbm,
-            ring, wdv, xv, gv, oa, nv, xnv, ss1, ss2, pown, prec, ysend, yrec, qown, qrec, qout,
-            s_in, s_wg, s_wu, s_wd, s_wo, s_wq, s_out,
+            xnv, qout,
+            ring, wdv, xv, gv, oa, nv, ss1, ss2, pown, prec, ysend, yrec, qown, qrec,
+            s_in, s_wg, s_wu, s_wd, s_wo, s_wq,
             c_ss, c_p, c_y_s, c_y_r, c_x_s, c_x_r, c_s2_s, c_s2_r, c_q):
     d, kd, ko, slots, half, ng, cw, ny, qw, nq, rows = cfg
     f, h = lax.axis_index('f'), lax.axis_index('h')
@@ -28,8 +28,8 @@
 
     def small():
         return [pltpu.make_async_copy(x_hbm, xv, s_in.at[0]),
-                pltpu.make_async_copy(g1_hbm, gv.at[pl.ds(0, 1)], s_in.at[1]),
-                pltpu.make_async_copy(g2_hbm, gv.at[pl.ds(1, 1)], s_in.at[2]),
+                pltpu.make_async_copy(g1_hbm, gv.at[0], s_in.at[1]),
+                pltpu.make_async_copy(g2_hbm, gv.at[1], s_in.at[2]),
                 pltpu.make_async_copy(o_hbm, oa.at[:, pl.ds(0, ko)], s_in.at[3])]
 
     def gu(j):
@@ -46,18 +46,21 @@
         slot, cols = lax.rem(j + ng, slots), pl.ds(pl.multiple_of(j * qw, 128), qw)
         return [pltpu.make_async_copy(wq_hbm.at[:, cols], ring.at[slot], s_wq.at[j])]
 
-    def start(copies):
+    def start(copies, priority):
         for c in copies:
-            c.start()
+            c.start(priority=priority)
 
     def wait(copies):
         for c in copies:
             c.wait()
 
+    def loop(lo, hi, fn):
+        lax.fori_loop(lo, hi, lambda i, _: (fn(i), 0)[1], 0)
+
     ins = small()
-    start(ins)
-    for j in range(slots):
-        start(gu(j))
+    start(ins, 0)
+    loop(0, slots, lambda j: start(gu(j), 0))
+    loop(0, ny, lambda c: start(dn(c), 1))
 
     barrier = pltpu.get_barrier_semaphore()
     for k in range(4):
@@ -74,7 +77,9 @@
     ex.start()
     ex.wait()
     r = lax.rsqrt((ss1[0] + ss1[1])[:, :1] / (2 * d) + EPS)
-    nv[...] = (xv[...].astype(F32) * r * gv[0:1, :]).astype(BF16)
+    for i in range(d // 128):
+        cols = slice(i * 128, (i + 1) * 128)
+        nv[:, cols] = (xv[:, cols].astype(F32) * r * gv[0, i:i + 1, :]).astype(BF16)
 
     def pcopy(j):
         return pltpu.make_async_remote_copy(pown.at[j], prec.at[j], c_p.at[0, j], c_p.at[1, j], partner, MESH)
@@ -92,23 +97,16 @@
 
         @pl.when(j + slots < ng)
         def _():
-            start(gu(j + slots))
-
-        @pl.when(j + slots == ng - 1)
+            start(gu(j + slots), 0)
+
+        @pl.when(j > 1)
         def _():
-            for c in range(ny):
-                start(dn(c))
-
-        @pl.when((j + slots >= ng) & (j + slots < ng + nq))
-        def _():
-            start(qk(j + slots - ng))
-
-        @pl.when(j > 0)
-        def _():
-            act(j - 1)
+            act(j - 2)
         return 0
 
     lax.fori_loop(0, ng, gu_step, 0)
+    loop(0, nq, lambda j: start(qk(j), 1))
+    act(ng - 2)
     act(ng - 1)
 
     def ycopy(c, k):
@@ -118,6 +116,7 @@
 
     def dn_step(c, _):
         wait(dn(c))
+
         ysend[c] = _dot(oa[...], wdv[c])
         for k in (3, 1, 2):
             ycopy(c, k).start()
@@ -162,34 +161,29 @@
     for c in range(ny):
         for k in (1, 2, 3):
             xcopy(c, k).wait_recv()
-        cols = slice(c * cw, (c + 1) * cw)
-        nv[:, cols] = (xnv[:, cols].astype(F32) * r * gv[1:2, cols]).astype(BF16)
-    xout = pltpu.make_async_copy(xnv, xo_hbm, s_out.at[nq])
-    xout.start()
+        for i in range(c * cw // 128, (c + 1) * cw // 128):
+            cols = slice(i * 128, (i + 1) * 128)
+            nv[:, cols] = (xnv[:, cols].astype(F32) * r * gv[1, i:i + 1, :]).astype(BF16)
 
     def qcopy(j):
         return pltpu.make_async_remote_copy(qown.at[j], qrec.at[j], c_q.at[0, j], c_q.at[1, j], partner, MESH)
-
-    def oput(j):
-        cols = pl.ds(pl.multiple_of(j * qw, 128), qw)
-        return pltpu.make_async_copy(qout.at[:, cols], qo_hbm.at[:, cols], s_out.at[j])
 
     def fin(j):
         qcopy(j).wait_recv()
         qout[:, pl.ds(pl.multiple_of(j * qw, 128), qw)] = (qown[j] + qrec[j]).astype(BF16)
-        oput(j).start()
 
     def q_step(j, _):
         wait(qk(j))
         qown[j] = _dot(nv[...], ring[lax.rem(j + ng, slots)])
         qcopy(j).start()
 
-        @pl.when(j > 0)
+        @pl.when(j > 1)
         def _():
-            fin(j - 1)
+            fin(j - 2)
         return 0
 
     lax.fori_loop(0, nq, q_step, 0)
+    fin(nq - 2)
     fin(nq - 1)
 
     for j in range(ng):
@@ -202,8 +196,15 @@
         scopy(k, t).wait_send()
     for j in range(nq):
         qcopy(j).wait_send()
-        oput(j).wait()
-    xout.wait()
+
+
+def _store(x_ref, q_ref, xo_hbm, qo_hbm, sem):
+    cx = pltpu.make_async_copy(x_ref, xo_hbm, sem.at[0])
+    cq = pltpu.make_async_copy(q_ref, qo_hbm, sem.at[1])
+    cx.start()
+    cq.start()
+    cx.wait()
+    cq.wait()
 
 
 def solution(mesh):
@@ -215,18 +216,20 @@
         cfg = (d, kd, ko, slots, half, ng, cw, ny, qw, nq, rows)
         dma = pltpu.SemaphoreType.DMA
         any_ = pl.BlockSpec(memory_space=pl.ANY)
-        return pl.pallas_call(
+        vmem = pl.BlockSpec(memory_space=pltpu.VMEM)
+        outs = (jax.ShapeDtypeStruct((t, d), BF16), jax.ShapeDtypeStruct((t, q), BF16))
+        mids = (pltpu.VMEM((t, d), BF16), pltpu.VMEM((t, q), BF16))
+        res = pl.pallas_call(
             functools.partial(_kernel, cfg),
-            out_shape=(jax.ShapeDtypeStruct((t, d), BF16), jax.ShapeDtypeStruct((t, q), BF16)),
+            out_shape=mids,
             in_specs=[any_] * 9,
-            out_specs=(any_, any_),
+            out_specs=(vmem, vmem),
             scratch_shapes=[
                 pltpu.VMEM((slots, d, 2 * half), BF16),
                 pltpu.VMEM((ny, ko + kd, cw), BF16),
                 pltpu.VMEM((t, d), BF16),
-                pltpu.VMEM((2, d), F32),
+                pltpu.VMEM((2, d // 128, 128), F32),
                 pltpu.VMEM((t, ko + kd), BF16),
-                pltpu.VMEM((t, d), BF16),
                 pltpu.VMEM((t, d), BF16),
                 pltpu.VMEM((2, t, 128), F32),
                 pltpu.VMEM((2, t, 128), F32),
@@ -236,15 +239,16 @@
                 pltpu.VMEM((3, ny, rows, cw), F32),
                 pltpu.VMEM((nq, t, qw), F32),
                 pltpu.VMEM((nq, t, qw), F32),
-                pltpu.VMEM((t, q), BF16),
-                dma((4,)), dma((ng,)), dma((ng,)), dma((ny,)), dma((ny,)), dma((nq,)), dma((nq + 1,)),
+                dma((4,)), dma((ng,)), dma((ng,)), dma((ny,)), dma((ny,)), dma((nq,)),
                 dma((2,)), dma((2, ng)), dma((3, ny)), dma((3, ny)), dma((3, ny)), dma((3, ny)),
                 dma((7,)), dma((7,)), dma((2, nq)),
             ],
             compiler_params=pltpu.CompilerParams(collective_id=0, has_side_effects=True,
-                                                 vmem_limit_bytes=66_000_000),
+                                                 vmem_limit_bytes=60_000_000),
             name='block',
-        )(x, g1.reshape(1, -1), g2.reshape(1, -1), w_gate, w_up, w_down, o, w_o, w_qkv)
+        )(x, g1.reshape(-1, 128), g2.reshape(-1, 128), w_gate, w_up, w_down, o, w_o, w_qkv)
+        return pl.pallas_call(_store, out_shape=outs, in_specs=[vmem, vmem], out_specs=(any_, any_),
+                              scratch_shapes=[dma((2,))], name='store')(*[pltpu.with_memory_space_constraint(r, pltpu.VMEM) for r in res])
 
     in_specs = (P(None, 'h'), P('h'), P('h'), P('h', 'f'), P('h', 'f'), P('f', 'h'),
                 P(None, 'f'), P('f', 'h'), P('h', 'f'))

time: 52.9 us -> 39.3 us (0.74)
  Pallas kernels: 45.8 us -> 38.5 us
  local copies, waits for them, and re-layouts: 6.18 us -> 0 us
    pallas_call x1 -> x2, Pallas kernels: 45.8 us -> 38.5 us  [the longest x1 37.6 us: body(): pl.pallas_call(functools.partial(_kernel, cfg), out_shape=mids, in_specs=...]
    unnamed x2 -> x0, local copies, waits for them, and re-layouts: 3.56 us -> none
    reshape x2 -> x0, local copies, waits for them, and re-layouts: 2.63 us -> none  [the longest x1 1.31 us: body(): g1.reshape(1, -1)]
where the time goes in v2:
time: 39.3 us; the launch traced here: 39.2 us
  Pallas kernels  38.5 us (98%)
  between operations  0.64 us (2%)
    pallas_call x1, Pallas kernels, body(): pl.pallas_call(functools.partial(_kernel, cfg), out_shape=mids, in_specs=...  37.6 us
    pallas_call x1, Pallas kernels, body(): pl.pallas_call(_store, out_shape=outs, in_specs=[vmem, vmem], out_specs=(...  0.91 us

profile of v2, /device:TPU:0, one launch (start us, length us, event | category | flops | bytes accessed | tf_op | source)
XLA Modules:
  0.0 39.2 jit_solution(11390362619195680416)
XLA Ops:
  0.6 37.6 %block.1 = (bf16[64,2560]{1,0:T(8,128)(2,1)S(1)}, bf16[64,3840]{1,0:T(8,128)(2,1)S(1)}) custom-call(bf16[64,2560]{1,0:T(8,128)(2,1)} %x_hbm.1, f32[20,128]{1,0:T(8,128)} %bitcast.2, f32[20,128]{1,0:T(8,128)} %bitcast.3, bf16[2560,3456]{1,0:T(8,128)(2,1)} %wg_hbm.1, bf16[2560,3456]{1,0:T(8,128)(2,1)} %wu_hbm.1, bf16[3456,2560]{1,0:T(8,128)(2,1)} %wd_hbm.1, ...), custom_call_target="tpu_custom_call" | custom-call | tf_op jit(solution)/shard_map/block/pallas_call | solution.py:222
  38.3 0.9 %store.1 = (bf16[64,2560]{1,0:T(8,128)(2,1)}, bf16[64,3840]{1,0:T(8,128)(2,1)}) custom-call(bf16[64,2560]{1,0:T(8,128)(2,1)S(1)} %get-tuple-element.4.x_ref, bf16[64,3840]{1,0:T(8,128)(2,1)S(1)} %get-tuple-element.5.q_ref), custom_call_target="tpu_custom_call" | custom-call | tf_op jit(solution)/shard_map/store/pallas_call | solution.py:250

commit v3 on v2

v3 whole, which is shorter than its diff:
```python
import functools

import jax
import jax.numpy as jnp
from jax import lax
from jax.experimental import pallas as pl
from jax.experimental.pallas import tpu as pltpu
from jax.sharding import PartitionSpec as P

EPS = 1e-6
MESH = pl.DeviceIdType.MESH
F32, BF16 = jnp.float32, jnp.bfloat16


def _dot(a, b):
    return jnp.dot(a, b, preferred_element_type=F32)


def _kernel(cfg, x_hbm, g1_hbm, g2_hbm, wg_hbm, wu_hbm, wd_hbm, o_hbm, wo_hbm, wq_hbm,
            xnv, qout,
            ring, wdv, xv, gv, oa, nv, ss1, ss2, pown, prec, ysend, yrec, qown, qrec,
            s_in, s_wg, s_wu, s_wd, s_wo, s_wq,
            c_ss, c_p, c_y, c_x, c_s2, c_q, c_sent):
    d, kd, ko, slots, half, ng, nl, cw, ny, qw, nq, rows = cfg
    f, h = lax.axis_index('f'), lax.axis_index('h')
    partner = (f, 1 - h)
    fx = [f, f + 1 - 2 * lax.rem(f, 2), lax.rem(f + 2, 4), 3 - f]

    def small():
        return [pltpu.make_async_copy(x_hbm, xv, s_in.at[0]),
                pltpu.make_async_copy(g1_hbm, gv.at[0], s_in.at[1]),
                pltpu.make_async_copy(g2_hbm, gv.at[1], s_in.at[2]),
                pltpu.make_async_copy(o_hbm, oa.at[:, pl.ds(0, ko)], s_in.at[3])]

    def gu(j):
        slot, cols = lax.rem(j, slots), pl.ds(pl.multiple_of(j * half, 128), half)
        return [pltpu.make_async_copy(wg_hbm.at[:, cols], ring.at[slot, :, pl.ds(0, half)], s_wg.at[j]),
                pltpu.make_async_copy(wu_hbm.at[:, cols], ring.at[slot, :, pl.ds(half, half)], s_wu.at[j])]

    def gl(e):
        cols = pl.ds(pl.multiple_of(ng * half + e * 128, 128), 128)
        lo, hi = pl.multiple_of(e * 256, 128), pl.multiple_of(e * 256 + 128, 128)
        return [pltpu.make_async_copy(wg_hbm.at[:, cols], ring.at[ng % slots, :, pl.ds(lo, 128)], s_wg.at[ng + e]),
                pltpu.make_async_copy(wu_hbm.at[:, cols], ring.at[ng % slots, :, pl.ds(hi, 128)], s_wu.at[ng + e])]

    def dn(c):
        cols = pl.ds(pl.multiple_of(c * cw, 128), cw)
        return [pltpu.make_async_copy(wo_hbm.at[:, cols], wdv.at[c, pl.ds(0, ko)], s_wo.at[c]),
                pltpu.make_async_copy(wd_hbm.at[:, cols], wdv.at[c, pl.ds(ko, kd)], s_wd.at[c])]

    def qk(j):
        slot, cols = lax.rem(j + ng + 1, slots), pl.ds(pl.multiple_of(j * qw, 128), qw)
        return [pltpu.make_async_copy(wq_hbm.at[:, cols], ring.at[slot], s_wq.at[j])]

    def took(ref, sem):
        pltpu.make_async_copy(ref, ref, sem).wait()

    def start(copies, priority):
        for c in copies:
            c.start(priority=priority)

    def wait(copies):
        for c in copies:
            c.wait()

    def loop(lo, hi, fn):
        lax.fori_loop(lo, hi, lambda i, _: (fn(i), 0)[1], 0)

    ins = small()
    start(ins, 0)
    loop(0, slots, lambda j: start(gu(j), 0))
    loop(0, ny, lambda c: start(dn(c), 1))

    barrier = pltpu.get_barrier_semaphore()
    for k in range(4):
        for t in range(2):
            if k or t:
                pl.semaphore_signal(barrier, inc=1, device_id=(fx[k], h if t == 0 else 1 - h), device_id_type=MESH)

    wait(ins)
    xf = xv[...].astype(F32)
    s = jnp.sum(xf * xf, axis=-1, keepdims=True)
    ss1[h] = jnp.broadcast_to(s, ss1.shape[1:])
    pl.semaphore_wait(barrier, 7)
    ex = pltpu.make_async_remote_copy(ss1.at[h], ss1.at[h], c_ss.at[0], c_ss.at[1], partner, MESH)
    ex.start()
    ex.wait()
    r = lax.rsqrt((ss1[0] + ss1[1])[:, :1] / (2 * d) + EPS)
    for i in range(d // 128):
        cols = slice(i * 128, (i + 1) * 128)
        nv[:, cols] = (xv[:, cols].astype(F32) * r * gv[0, i:i + 1, :]).astype(BF16)

    def pcopy(j):
        return pltpu.make_async_remote_copy(pown.at[j], prec.at[j], c_sent.at[0], c_p.at[j], partner, MESH)

    def lcopy(e):
        part = pl.ds(pl.multiple_of(e * 256, 128), 256)
        return pltpu.make_async_remote_copy(pown.at[ng, :, part], prec.at[ng, :, part], c_sent.at[1], c_p.at[ng + e],
                                            partner, MESH)

    def silu_mul(g, u):
        return (g / (1.0 + jnp.exp(-g)) * u).astype(BF16)

    def act(j):
        pcopy(j).wait_recv()
        oa[:, pl.ds(pl.multiple_of(ko + j * half, 128), half)] = silu_mul(pown[j, :, :half] + prec[j, :, :half],
                                                                          pown[j, :, half:] + prec[j, :, half:])

    def last_act(e):
        lcopy(e).wait_recv()
        lo, hi = (pl.ds(pl.multiple_of(e * 256 + i, 128), 128) for i in (0, 128))
        oa[:, pl.ds(pl.multiple_of(ko + ng * half + e * 128, 128), 128)] = silu_mul(
            pown[ng, :, lo] + prec[ng, :, lo], pown[ng, :, hi] + prec[ng, :, hi])

    def gu_step(j, _):
        wait(gu(j))
        pown[j] = _dot(nv[...], ring[lax.rem(j, slots)])
        pcopy(j).start()

        @pl.when(j + slots < ng)
        def _():
            start(gu(j + slots), 0)

        @pl.when(j + slots == ng)
        def _():
            loop(0, nl, lambda e: start(gl(e), 0))

        @pl.when(j > 1)
        def _():
            act(j - 2)
        return 0

    def gl_step(e, _):
        wait(gl(e))
        part = pl.ds(pl.multiple_of(e * 256, 128), 256)
        pown[ng, :, part] = _dot(nv[...], ring[ng % slots, :, part])
        lcopy(e).start()
        return 0

    lax.fori_loop(0, ng, gu_step, 0)
    lax.fori_loop(0, nl, gl_step, 0)
    loop(0, nq, lambda j: start(qk(j), 1))

    blk = [pl.ds(pl.multiple_of(fx[k] * rows, rows), rows) for k in range(4)]
    mine = blk[0]

    def chunk(c):
        return pl.ds(pl.multiple_of(c * cw, 128), cw)

    def ycopy(c, k):
        return pltpu.make_async_remote_copy(ysend.at[c, blk[k]], yrec.at[k - 1, c], c_sent.at[2], c_y.at[c],
                                            (fx[k], h), MESH)

    def xcopy(c, k):
        return pltpu.make_async_remote_copy(xnv.at[mine, chunk(c)], xnv.at[mine, chunk(c)], c_sent.at[3],
                                            c_x.at[0], (fx[k], h), MESH)

    def scatter(c):
        for k in (3, 1, 2):
            ycopy(c, k).start()

    act(ng - 2)
    wait(dn(0))
    kk = ko + (ng - 1) * half
    ysend[0] = _dot(oa[:, :kk], wdv[0, :kk])
    act(ng - 1)
    loop(0, nl, last_act)
    ysend[0] = ysend[0] + _dot(oa[:, kk:], wdv[0, kk:])
    scatter(0)

    def dn_step(c, _):
        wait(dn(c))
        ysend[c] = _dot(oa[...], wdv[c])
        scatter(c)
        return 0

    lax.fori_loop(1, ny, dn_step, 0)

    def block(c, s):
        took(yrec.at[:, c], c_y.at[c])
        y = (ysend[c, mine] + yrec[0, c]) + (yrec[1, c] + yrec[2, c])
        xn = (xv[mine, chunk(c)].astype(F32) + y).astype(BF16)
        xnv[mine, chunk(c)] = xn

        @pl.when(c < ny - 2)
        def _():
            for k in (3, 1, 2):
                xcopy(c, k).start()

        xf = xn.astype(F32)
        return s + jnp.sum(xf * xf, axis=-1, keepdims=True)

    s = lax.fori_loop(0, ny, block, jnp.zeros((rows, 1), F32))

    def diag(n, first):
        i = lax.broadcasted_iota(jnp.int32, (n, 128), 0) + first
        return i == lax.broadcasted_iota(jnp.int32, (n, 128), 1)

    ss2[h * 4 + f] = jnp.sum(jnp.where(diag(rows, f * rows), s, 0.0), axis=0, keepdims=True)

    def scopy(k, t):
        return pltpu.make_async_remote_copy(ss2.at[h * 4 + f], ss2.at[h * 4 + f], c_sent.at[5], c_s2.at[0],
                                            (fx[k], h if t == 0 else 1 - h), MESH)

    peers = [(k, t) for k in (3, 1, 2, 0) for t in (0, 1) if k or t]
    for k, t in peers:
        scopy(k, t).start()
    for c in (ny - 2, ny - 1):
        for k in (3, 1, 2):
            xcopy(c, k).start()
    took(pown.at[pl.ds(0, ng)], c_sent.at[0])
    took(pown.at[ng], c_sent.at[1])
    took(ysend.at[:, pl.ds(0, 3 * rows)], c_sent.at[2])
    took(ss2.at[pl.ds(0, 7)], c_sent.at[5])
    took(ss2.at[pl.ds(0, 7)], c_s2.at[0])
    tot = sum(ss2[i] + ss2[4 + i] for i in range(4))
    tot = jnp.sum(jnp.where(diag(4 * rows, 0), tot, 0.0), axis=1, keepdims=True)
    r = lax.rsqrt(tot / (2 * d) + EPS)

    took(xnv.at[pl.ds(0, 3 * rows)], c_x.at[0])

    def renorm(c):
        for i in range(cw // 128):
            cols = pl.ds(pl.multiple_of(c * cw + i * 128, 128), 128)
            nv[:, cols] = (xnv[:, cols].astype(F32) * r * gv[1, pl.ds(c * (cw // 128) + i, 1), :]).astype(BF16)

    loop(0, ny, renorm)

    def qcopy(j):
        return pltpu.make_async_remote_copy(qown.at[j], qrec.at[j], c_sent.at[4], c_q.at[j], partner, MESH)

    def fin(j):
        qcopy(j).wait_recv()
        qout[:, pl.ds(pl.multiple_of(j * qw, 128), qw)] = (qown[j] + qrec[j]).astype(BF16)

    def q_pair(i, _):
        wait(qk(2 * i) + qk(2 * i + 1))
        for j in (2 * i, 2 * i + 1):
            qown[j] = _dot(nv[...], ring[lax.rem(j + ng + 1, slots)])
        for j in (2 * i, 2 * i + 1):
            qcopy(j).start()

        @pl.when(i > 0)
        def _():
            fin(2 * i - 2)
            fin(2 * i - 1)
        return 0

    lax.fori_loop(0, nq // 2, q_pair, 0)
    wait(qk(nq - 1))
    qown[nq - 1] = _dot(nv[...], ring[(nq + ng) % slots])
    qcopy(nq - 1).start()
    for j in range(nq - 3, nq):
        fin(j)

    took(xnv.at[pl.ds(0, 3 * rows)], c_sent.at[3])
    took(qown, c_sent.at[4])


def _store(x_ref, q_ref, xo_hbm, qo_hbm, sem):
    cx = pltpu.make_async_copy(x_ref, xo_hbm, sem.at[0])
    cq = pltpu.make_async_copy(q_ref, qo_hbm, sem.at[1])
    cx.start()
    cq.start()
    cx.wait()
    cq.wait()


def solution(mesh):
    def body(x, g1, g2, w_gate, w_up, w_down, o, w_o, w_qkv):
        t, d = x.shape
        kd, ko, q = w_down.shape[0], w_o.shape[0], w_qkv.shape[1]
        slots, half, nl, cw, qw = 6, 384, 3, 256, 768
        ng, ny, nq, rows = kd // half - 1, d // cw, q // qw, t // 4
        cfg = (d, kd, ko, slots, half, ng, nl, cw, ny, qw, nq, rows)
        dma = pltpu.SemaphoreType.DMA
        any_ = pl.BlockSpec(memory_space=pl.ANY)
        vmem = pl.BlockSpec(memory_space=pltpu.VMEM)
        outs = (jax.ShapeDtypeStruct((t, d), BF16), jax.ShapeDtypeStruct((t, q), BF16))
        mids = (pltpu.VMEM((t, d), BF16), pltpu.VMEM((t, q), BF16))
        res = pl.pallas_call(
            functools.partial(_kernel, cfg),
            out_shape=mids,
            in_specs=[any_] * 9,
            out_specs=(vmem, vmem),
            scratch_shapes=[
                pltpu.VMEM((slots, d, 2 * half), BF16),
                pltpu.VMEM((ny, ko + kd, cw), BF16),
                pltpu.VMEM((t, d), BF16),
                pltpu.VMEM((2, d // 128, 128), F32),
                pltpu.VMEM((t, ko + kd), BF16),
                pltpu.VMEM((t, d), BF16),
                pltpu.VMEM((2, t, 128), F32),
                pltpu.VMEM((8, 1, 128), F32),
                pltpu.VMEM((ng + 1, t, 2 * half), F32),
                pltpu.VMEM((ng + 1, t, 2 * half), F32),
                pltpu.VMEM((ny, t, cw), F32),
                pltpu.VMEM((3, ny, rows, cw), F32),
                pltpu.VMEM((nq, t, qw), F32),
                pltpu.VMEM((nq, t, qw), F32),
                dma((4,)), dma((ng + nl,)), dma((ng + nl,)), dma((ny,)), dma((ny,)), dma((nq,)),
                dma((2,)), dma((ng + nl,)), dma((ny,)), dma((1,)), dma((1,)), dma((nq,)), dma((6,)),
            ],
            compiler_params=pltpu.CompilerParams(collective_id=0, has_side_effects=True,
                                                 vmem_limit_bytes=60_000_000),
            name='block',
        )(x, g1.reshape(-1, 128), g2.reshape(-1, 128), w_gate, w_up, w_down, o, w_o, w_qkv)
        return pl.pallas_call(_store, out_shape=outs, in_specs=[vmem, vmem], out_specs=(any_, any_),
                              scratch_shapes=[dma((2,))], name='store')(*[pltpu.with_memory_space_constraint(r, pltpu.VMEM) for r in res])

    in_specs = (P(None, 'h'), P('h'), P('h'), P('h', 'f'), P('h', 'f'), P('f', 'h'),
                P(None, 'f'), P('f', 'h'), P('h', 'f'))
    return jax.shard_map(body, mesh=mesh, in_specs=in_specs,
                         out_specs=(P(None, 'h'), P(None, 'f')), check_vma=False)
```

time: 39.3 us -> 37.4 us (0.952)
  Pallas kernels: 38.5 us -> 36.7 us
    pallas_call x1, Pallas kernels: 37.6 us -> 35.8 us  [body(): pl.pallas_call(functools.partial(_kernel, cfg), out_shape=mids, in_specs=...]
where the time goes in v3:
time: 37.4 us; the launch traced here: 37.3 us
  Pallas kernels  36.7 us (98%)
  between operations  0.64 us (2%)
    pallas_call x1, Pallas kernels, body(): pl.pallas_call(functools.partial(_kernel, cfg), out_shape=mids, in_specs=...  35.8 us
    pallas_call x1, Pallas kernels, body(): pl.pallas_call(_store, out_shape=outs, in_specs=[vmem, vmem], out_specs=(...  0.91 us

profile of v3, /device:TPU:0, one launch (start us, length us, event | category | flops | bytes accessed | tf_op | source)
XLA Modules:
  0.0 37.3 jit_solution(11453157030729799789)
XLA Ops:
  0.6 35.8 %block.1 = (bf16[64,2560]{1,0:T(8,128)(2,1)S(1)}, bf16[64,3840]{1,0:T(8,128)(2,1)S(1)}) custom-call(bf16[64,2560]{1,0:T(8,128)(2,1)} %x_hbm.1, f32[20,128]{1,0:T(8,128)} %bitcast.2, f32[20,128]{1,0:T(8,128)} %bitcast.3, bf16[2560,3456]{1,0:T(8,128)(2,1)} %wg_hbm.1, bf16[2560,3456]{1,0:T(8,128)(2,1)} %wu_hbm.1, bf16[3456,2560]{1,0:T(8,128)(2,1)} %wd_hbm.1, ...), custom_call_target="tpu_custom_call" | custom-call | tf_op jit(solution)/shard_map/block/pallas_call | solution.py:281
  36.4 0.9 %store.1 = (bf16[64,2560]{1,0:T(8,128)(2,1)}, bf16[64,3840]{1,0:T(8,128)(2,1)}) custom-call(bf16[64,2560]{1,0:T(8,128)(2,1)S(1)} %get-tuple-element.4.x_ref, bf16[64,3840]{1,0:T(8,128)(2,1)S(1)} %get-tuple-element.5.q_ref), custom_call_target="tpu_custom_call" | custom-call | tf_op jit(solution)/shard_map/store/pallas_call | solution.py:308

commit v4 on v3

--- a/solution.py
+++ b/solution.py
@@ -19,7 +19,7 @@
 def _kernel(cfg, x_hbm, g1_hbm, g2_hbm, wg_hbm, wu_hbm, wd_hbm, o_hbm, wo_hbm, wq_hbm,
             xnv, qout,
             ring, wdv, xv, gv, oa, nv, ss1, ss2, pown, prec, ysend, yrec, qown, qrec,
-            s_in, s_wg, s_wu, s_wd, s_wo, s_wq,
+            s_in, s_w, s_dn,
             c_ss, c_p, c_y, c_x, c_s2, c_q, c_sent):
     d, kd, ko, slots, half, ng, nl, cw, ny, qw, nq, rows = cfg
     f, h = lax.axis_index('f'), lax.axis_index('h')
@@ -29,28 +29,28 @@
     def small():
         return [pltpu.make_async_copy(x_hbm, xv, s_in.at[0]),
                 pltpu.make_async_copy(g1_hbm, gv.at[0], s_in.at[1]),
-                pltpu.make_async_copy(g2_hbm, gv.at[1], s_in.at[2]),
-                pltpu.make_async_copy(o_hbm, oa.at[:, pl.ds(0, ko)], s_in.at[3])]
+                pltpu.make_async_copy(g2_hbm, gv.at[1], s_in.at[1]),
+                pltpu.make_async_copy(o_hbm, oa.at[:, pl.ds(0, ko)], s_in.at[2])]
 
     def gu(j):
         slot, cols = lax.rem(j, slots), pl.ds(pl.multiple_of(j * half, 128), half)
-        return [pltpu.make_async_copy(wg_hbm.at[:, cols], ring.at[slot, :, pl.ds(0, half)], s_wg.at[j]),
-                pltpu.make_async_copy(wu_hbm.at[:, cols], ring.at[slot, :, pl.ds(half, half)], s_wu.at[j])]
+        return [pltpu.make_async_copy(wg_hbm.at[:, cols], ring.at[slot, :, pl.ds(0, half)], s_w.at[slot]),
+                pltpu.make_async_copy(wu_hbm.at[:, cols], ring.at[slot, :, pl.ds(half, half)], s_w.at[slot])]
 
     def gl(e):
         cols = pl.ds(pl.multiple_of(ng * half + e * 128, 128), 128)
         lo, hi = pl.multiple_of(e * 256, 128), pl.multiple_of(e * 256 + 128, 128)
-        return [pltpu.make_async_copy(wg_hbm.at[:, cols], ring.at[ng % slots, :, pl.ds(lo, 128)], s_wg.at[ng + e]),
-                pltpu.make_async_copy(wu_hbm.at[:, cols], ring.at[ng % slots, :, pl.ds(hi, 128)], s_wu.at[ng + e])]
+        return [pltpu.make_async_copy(wg_hbm.at[:, cols], ring.at[ng % slots, :, pl.ds(lo, 128)], s_w.at[slots + e]),
+                pltpu.make_async_copy(wu_hbm.at[:, cols], ring.at[ng % slots, :, pl.ds(hi, 128)], s_w.at[slots + e])]
 
     def dn(c):
         cols = pl.ds(pl.multiple_of(c * cw, 128), cw)
-        return [pltpu.make_async_copy(wo_hbm.at[:, cols], wdv.at[c, pl.ds(0, ko)], s_wo.at[c]),
-                pltpu.make_async_copy(wd_hbm.at[:, cols], wdv.at[c, pl.ds(ko, kd)], s_wd.at[c])]
+        return [pltpu.make_async_copy(wo_hbm.at[:, cols], wdv.at[c, pl.ds(0, ko)], s_dn.at[c]),
+                pltpu.make_async_copy(wd_hbm.at[:, cols], wdv.at[c, pl.ds(ko, kd)], s_dn.at[c])]
 
     def qk(j):
         slot, cols = lax.rem(j + ng + 1, slots), pl.ds(pl.multiple_of(j * qw, 128), qw)
-        return [pltpu.make_async_copy(wq_hbm.at[:, cols], ring.at[slot], s_wq.at[j])]
+        return [pltpu.make_async_copy(wq_hbm.at[:, cols], ring.at[slot], s_w.at[slot])]
 
     def took(ref, sem):
         pltpu.make_async_copy(ref, ref, sem).wait()
@@ -77,7 +77,7 @@
             if k or t:
                 pl.semaphore_signal(barrier, inc=1, device_id=(fx[k], h if t == 0 else 1 - h), device_id_type=MESH)
 
-    wait(ins)
+    took(xv, s_in.at[0])
     xf = xv[...].astype(F32)
     s = jnp.sum(xf * xf, axis=-1, keepdims=True)
     ss1[h] = jnp.broadcast_to(s, ss1.shape[1:])
@@ -86,6 +86,7 @@
     ex.start()
     ex.wait()
     r = lax.rsqrt((ss1[0] + ss1[1])[:, :1] / (2 * d) + EPS)
+    took(gv, s_in.at[1])
     for i in range(d // 128):
         cols = slice(i * 128, (i + 1) * 128)
         nv[:, cols] = (xv[:, cols].astype(F32) * r * gv[0, i:i + 1, :]).astype(BF16)
@@ -95,7 +96,7 @@
 
     def lcopy(e):
         part = pl.ds(pl.multiple_of(e * 256, 128), 256)
-        return pltpu.make_async_remote_copy(pown.at[ng, :, part], prec.at[ng, :, part], c_sent.at[1], c_p.at[ng + e],
+        return pltpu.make_async_remote_copy(pown.at[ng, :, part], prec.at[ng, :, part], c_sent.at[0], c_p.at[ng],
                                             partner, MESH)
 
     def silu_mul(g, u):
@@ -107,13 +108,12 @@
                                                                           pown[j, :, half:] + prec[j, :, half:])
 
     def last_act(e):
-        lcopy(e).wait_recv()
         lo, hi = (pl.ds(pl.multiple_of(e * 256 + i, 128), 128) for i in (0, 128))
         oa[:, pl.ds(pl.multiple_of(ko + ng * half + e * 128, 128), 128)] = silu_mul(
             pown[ng, :, lo] + prec[ng, :, lo], pown[ng, :, hi] + prec[ng, :, hi])
 
     def gu_step(j, _):
-        wait(gu(j))
+        took(ring.at[lax.rem(j, slots)], s_w.at[lax.rem(j, slots)])
         pown[j] = _dot(nv[...], ring[lax.rem(j, slots)])
         pcopy(j).start()
 
@@ -131,8 +131,8 @@
         return 0
 
     def gl_step(e, _):
-        wait(gl(e))
         part = pl.ds(pl.multiple_of(e * 256, 128), 256)
+        took(ring.at[ng % slots, :, part], s_w.at[slots + e])
         pown[ng, :, part] = _dot(nv[...], ring[ng % slots, :, part])
         lcopy(e).start()
         return 0
@@ -148,28 +148,34 @@
         return pl.ds(pl.multiple_of(c * cw, 128), cw)
 
     def ycopy(c, k):
-        return pltpu.make_async_remote_copy(ysend.at[c, blk[k]], yrec.at[k - 1, c], c_sent.at[2], c_y.at[c],
+        return pltpu.make_async_remote_copy(ysend.at[c, blk[k]], yrec.at[k - 1, c], c_sent.at[1], c_y.at[c],
                                             (fx[k], h), MESH)
 
     def xcopy(c, k):
-        return pltpu.make_async_remote_copy(xnv.at[mine, chunk(c)], xnv.at[mine, chunk(c)], c_sent.at[3],
-                                            c_x.at[0], (fx[k], h), MESH)
+        at = xnv.at[mine, chunk(c)]
+        return pltpu.make_async_remote_copy(at, at, c_sent.at[2], c_x.at[lax.div(c, ny // 2)], (fx[k], h), MESH)
+
+    def spread(c):
+        for k in (3, 1, 2):
+            xcopy(c, k).start()
 
     def scatter(c):
         for k in (3, 1, 2):
             ycopy(c, k).start()
 
     act(ng - 2)
-    wait(dn(0))
+    ins[3].wait()
+    took(wdv.at[0], s_dn.at[0])
     kk = ko + (ng - 1) * half
     ysend[0] = _dot(oa[:, :kk], wdv[0, :kk])
     act(ng - 1)
+    took(prec.at[ng], c_p.at[ng])
     loop(0, nl, last_act)
     ysend[0] = ysend[0] + _dot(oa[:, kk:], wdv[0, kk:])
     scatter(0)
 
     def dn_step(c, _):
-        wait(dn(c))
+        took(wdv.at[c], s_dn.at[c])
         ysend[c] = _dot(oa[...], wdv[c])
         scatter(c)
         return 0
@@ -182,10 +188,9 @@
         xn = (xv[mine, chunk(c)].astype(F32) + y).astype(BF16)
         xnv[mine, chunk(c)] = xn
 
-        @pl.when(c < ny - 2)
+        @pl.when(c < ny // 2)
         def _():
-            for k in (3, 1, 2):
-                xcopy(c, k).start()
+            spread(c)
 
         xf = xn.astype(F32)
         return s + jnp.sum(xf * xf, axis=-1, keepdims=True)
@@ -199,62 +204,74 @@
     ss2[h * 4 + f] = jnp.sum(jnp.where(diag(rows, f * rows), s, 0.0), axis=0, keepdims=True)
 
     def scopy(k, t):
-        return pltpu.make_async_remote_copy(ss2.at[h * 4 + f], ss2.at[h * 4 + f], c_sent.at[5], c_s2.at[0],
+        return pltpu.make_async_remote_copy(ss2.at[h * 4 + f], ss2.at[h * 4 + f], c_sent.at[4], c_s2.at[0],
                                             (fx[k], h if t == 0 else 1 - h), MESH)
 
     peers = [(k, t) for k in (3, 1, 2, 0) for t in (0, 1) if k or t]
     for k, t in peers:
         scopy(k, t).start()
-    for c in (ny - 2, ny - 1):
-        for k in (3, 1, 2):
-            xcopy(c, k).start()
-    took(pown.at[pl.ds(0, ng)], c_sent.at[0])
-    took(pown.at[ng], c_sent.at[1])
-    took(ysend.at[:, pl.ds(0, 3 * rows)], c_sent.at[2])
-    took(ss2.at[pl.ds(0, 7)], c_sent.at[5])
+    loop(ny // 2, ny, spread)
+    qown[...] = jnp.zeros_like(qown)
+    took(pown, c_sent.at[0])
+    took(ysend.at[:, pl.ds(0, 3 * rows)], c_sent.at[1])
+    took(ss2.at[pl.ds(0, 7)], c_sent.at[4])
     took(ss2.at[pl.ds(0, 7)], c_s2.at[0])
     tot = sum(ss2[i] + ss2[4 + i] for i in range(4))
     tot = jnp.sum(jnp.where(diag(4 * rows, 0), tot, 0.0), axis=1, keepdims=True)
     r = lax.rsqrt(tot / (2 * d) + EPS)
 
-    took(xnv.at[pl.ds(0, 3 * rows)], c_x.at[0])
 
     def renorm(c):
         for i in range(cw // 128):
             cols = pl.ds(pl.multiple_of(c * cw + i * 128, 128), 128)
             nv[:, cols] = (xnv[:, cols].astype(F32) * r * gv[1, pl.ds(c * (cw // 128) + i, 1), :]).astype(BF16)
 
-    loop(0, ny, renorm)
-
     def qcopy(j):
-        return pltpu.make_async_remote_copy(qown.at[j], qrec.at[j], c_sent.at[4], c_q.at[j], partner, MESH)
+        return pltpu.make_async_remote_copy(qown.at[j], qrec.at[j], c_sent.at[3], c_q.at[lax.div(j, 2)], partner, MESH)
 
     def fin(j):
-        qcopy(j).wait_recv()
         qout[:, pl.ds(pl.multiple_of(j * qw, 128), qw)] = (qown[j] + qrec[j]).astype(BF16)
 
-    def q_pair(i, _):
-        wait(qk(2 * i) + qk(2 * i + 1))
-        for j in (2 * i, 2 * i + 1):
-            qown[j] = _dot(nv[...], ring[lax.rem(j + ng + 1, slots)])
-        for j in (2 * i, 2 * i + 1):
-            qcopy(j).start()
-
-        @pl.when(i > 0)
-        def _():
-            fin(2 * i - 2)
-            fin(2 * i - 1)
+    def q_pass(p, _):
+        took(xnv.at[pl.ds(0, 3 * rows), pl.ds(0, d // 2)], c_x.at[p])
+        loop(p * (ny // 2), (p + 1) * (ny // 2), renorm)
+        ks = pl.ds(pl.multiple_of(p * (d // 2), 128), d // 2)
+
+        def add(*js):
+            @pl.when(p == 0)
+            def _():
+                for j in js:
+                    wait(qk(j))
+
+            for j in js:
+                qown[j] = qown[j] + _dot(nv[:, ks], ring[lax.rem(j + ng + 1, slots), ks])
+
+            @pl.when(p == 1)
+            def _():
+                for j in js:
+                    qcopy(j).start()
+
+        def q_pair(i, _):
+            add(2 * i, 2 * i + 1)
+            return 0
+
+        lax.fori_loop(0, nq // 2, q_pair, 0)
+        add(nq - 1)
         return 0
 
-    lax.fori_loop(0, nq // 2, q_pair, 0)
-    wait(qk(nq - 1))
-    qown[nq - 1] = _dot(nv[...], ring[(nq + ng) % slots])
-    qcopy(nq - 1).start()
-    for j in range(nq - 3, nq):
-        fin(j)
-
-    took(xnv.at[pl.ds(0, 3 * rows)], c_sent.at[3])
-    took(qown, c_sent.at[4])
+    lax.fori_loop(0, 2, q_pass, 0)
+
+    def fin_pair(i):
+        took(qrec.at[pl.ds(0, 2)], c_q.at[i])
+        fin(2 * i)
+        fin(2 * i + 1)
+
+    loop(0, nq // 2, fin_pair)
+    took(qrec.at[0], c_q.at[nq // 2])
+    fin(nq - 1)
+
+    took(xnv.at[pl.ds(0, 3 * rows)], c_sent.at[2])
+    took(qown, c_sent.at[3])
 
 
 def _store(x_ref, q_ref, xo_hbm, qo_hbm, sem):
@@ -298,8 +315,8 @@
                 pltpu.VMEM((3, ny, rows, cw), F32),
                 pltpu.VMEM((nq, t, qw), F32),
                 pltpu.VMEM((nq, t, qw), F32),
-                dma((4,)), dma((ng + nl,)), dma((ng + nl,)), dma((ny,)), dma((ny,)), dma((nq,)),
-                dma((2,)), dma((ng + nl,)), dma((ny,)), dma((1,)), dma((1,)), dma((nq,)), dma((6,)),
+                dma((3,)), dma((slots + nl,)), dma((ny,)),
+                dma((2,)), dma((ng + 1,)), dma((ny,)), dma((2,)), dma((1,)), dma(((nq + 1) // 2,)), dma((5,)),
             ],
             compiler_params=pltpu.CompilerParams(collective_id=0, has_side_effects=True,
                                                  vmem_limit_bytes=60_000_000),

time: 37.4 us -> 36.6 us (0.979)
  Pallas kernels: 36.7 us -> 35.8 us
    pallas_call x1, Pallas kernels: 35.8 us -> 34.9 us  [body(): pl.pallas_call(functools.partial(_kernel, cfg), out_shape=mids, in_specs=...]
where the time goes in v4:
time: 36.6 us; the launch traced here: 36.5 us
  Pallas kernels  35.8 us (98%)
  between operations  0.64 us (2%)
    pallas_call x1, Pallas kernels, body(): pl.pallas_call(functools.partial(_kernel, cfg), out_shape=mids, in_specs=...  34.9 us
    pallas_call x1, Pallas kernels, body(): pl.pallas_call(_store, out_shape=outs, in_specs=[vmem, vmem], out_specs=(...  0.91 us

profile of v4, /device:TPU:0, one launch (start us, length us, event | category | flops | bytes accessed | tf_op | source)
XLA Modules:
  0.0 36.5 jit_solution(17654897423095109369)
XLA Ops:
  0.6 34.9 %block.1 = (bf16[64,2560]{1,0:T(8,128)(2,1)S(1)}, bf16[64,3840]{1,0:T(8,128)(2,1)S(1)}) custom-call(bf16[64,2560]{1,0:T(8,128)(2,1)} %x_hbm.1, f32[20,128]{1,0:T(8,128)} %bitcast.2, f32[20,128]{1,0:T(8,128)} %bitcast.3, bf16[2560,3456]{1,0:T(8,128)(2,1)} %wg_hbm.1, bf16[2560,3456]{1,0:T(8,128)(2,1)} %wu_hbm.1, bf16[3456,2560]{1,0:T(8,128)(2,1)} %wd_hbm.1, ...), custom_call_target="tpu_custom_call" | custom-call | tf_op jit(solution)/shard_map/block/pallas_call | solution.py:298
  35.6 0.9 %store.1 = (bf16[64,2560]{1,0:T(8,128)(2,1)}, bf16[64,3840]{1,0:T(8,128)(2,1)}) custom-call(bf16[64,2560]{1,0:T(8,128)(2,1)S(1)} %get-tuple-element.4.x_ref, bf16[64,3840]{1,0:T(8,128)(2,1)S(1)} %get-tuple-element.5.q_ref), custom_call_target="tpu_custom_call" | custom-call | tf_op jit(solution)/shard_map/store/pallas_call | solution.py:325

commit v5 on v4

--- a/solution.py
+++ b/solution.py
@@ -21,7 +21,7 @@
             ring, wdv, xv, gv, oa, nv, ss1, ss2, pown, prec, ysend, yrec, qown, qrec,
             s_in, s_w, s_dn,
             c_ss, c_p, c_y, c_x, c_s2, c_q, c_sent):
-    d, kd, ko, slots, half, ng, nl, cw, ny, qw, nq, rows = cfg
+    d, kd, ko, slots, half, ng, nm, cw, ny, qw, nq, rows = cfg
     f, h = lax.axis_index('f'), lax.axis_index('h')
     partner = (f, 1 - h)
     fx = [f, f + 1 - 2 * lax.rem(f, 2), lax.rem(f + 2, 4), 3 - f]
@@ -32,16 +32,18 @@
                 pltpu.make_async_copy(g2_hbm, gv.at[1], s_in.at[1]),
                 pltpu.make_async_copy(o_hbm, oa.at[:, pl.ds(0, ko)], s_in.at[2])]
 
-    def gu(j):
-        slot, cols = lax.rem(j, slots), pl.ds(pl.multiple_of(j * half, 128), half)
-        return [pltpu.make_async_copy(wg_hbm.at[:, cols], ring.at[slot, :, pl.ds(0, half)], s_w.at[slot]),
-                pltpu.make_async_copy(wu_hbm.at[:, cols], ring.at[slot, :, pl.ds(half, half)], s_w.at[slot])]
-
-    def gl(e):
-        cols = pl.ds(pl.multiple_of(ng * half + e * 128, 128), 128)
-        lo, hi = pl.multiple_of(e * 256, 128), pl.multiple_of(e * 256 + 128, 128)
-        return [pltpu.make_async_copy(wg_hbm.at[:, cols], ring.at[ng % slots, :, pl.ds(lo, 128)], s_w.at[slots + e]),
-                pltpu.make_async_copy(wu_hbm.at[:, cols], ring.at[ng % slots, :, pl.ds(hi, 128)], s_w.at[slots + e])]
+    def wide(j):
+        return j, pl.multiple_of(j * half, 128), half
+
+    def mid(m):
+        return ng + m, pl.multiple_of(ng * half + m * 256, 128), 256
+
+    last = (ng + nm, ng * half + nm * 256, 128)
+
+    def gu(i, at, w):
+        slot, cols = lax.rem(i, slots), pl.ds(at, w)
+        return [pltpu.make_async_copy(wg_hbm.at[:, cols], ring.at[slot, :, pl.ds(0, w)], s_w.at[slot]),
+                pltpu.make_async_copy(wu_hbm.at[:, cols], ring.at[slot, :, pl.ds(w, w)], s_w.at[slot])]
 
     def dn(c):
         cols = pl.ds(pl.multiple_of(c * cw, 128), cw)
@@ -49,7 +51,7 @@
                 pltpu.make_async_copy(wd_hbm.at[:, cols], wdv.at[c, pl.ds(ko, kd)], s_dn.at[c])]
 
     def qk(j):
-        slot, cols = lax.rem(j + ng + 1, slots), pl.ds(pl.multiple_of(j * qw, 128), qw)
+        slot, cols = lax.rem(j + ng + nm + 1, slots), pl.ds(pl.multiple_of(j * qw, 128), qw)
         return [pltpu.make_async_copy(wq_hbm.at[:, cols], ring.at[slot], s_w.at[slot])]
 
     def took(ref, sem):
@@ -68,7 +70,7 @@
 
     ins = small()
     start(ins, 0)
-    loop(0, slots, lambda j: start(gu(j), 0))
+    loop(0, ng, lambda j: start(gu(*wide(j)), 0))
     loop(0, ny, lambda c: start(dn(c), 1))
 
     barrier = pltpu.get_barrier_semaphore()
@@ -91,54 +93,50 @@
         cols = slice(i * 128, (i + 1) * 128)
         nv[:, cols] = (xv[:, cols].astype(F32) * r * gv[0, i:i + 1, :]).astype(BF16)
 
-    def pcopy(j):
-        return pltpu.make_async_remote_copy(pown.at[j], prec.at[j], c_sent.at[0], c_p.at[j], partner, MESH)
-
-    def lcopy(e):
-        part = pl.ds(pl.multiple_of(e * 256, 128), 256)
-        return pltpu.make_async_remote_copy(pown.at[ng, :, part], prec.at[ng, :, part], c_sent.at[0], c_p.at[ng],
-                                            partner, MESH)
-
-    def silu_mul(g, u):
-        return (g / (1.0 + jnp.exp(-g)) * u).astype(BF16)
-
-    def act(j):
-        pcopy(j).wait_recv()
-        oa[:, pl.ds(pl.multiple_of(ko + j * half, 128), half)] = silu_mul(pown[j, :, :half] + prec[j, :, :half],
-                                                                          pown[j, :, half:] + prec[j, :, half:])
-
-    def last_act(e):
-        lo, hi = (pl.ds(pl.multiple_of(e * 256 + i, 128), 128) for i in (0, 128))
-        oa[:, pl.ds(pl.multiple_of(ko + ng * half + e * 128, 128), 128)] = silu_mul(
-            pown[ng, :, lo] + prec[ng, :, lo], pown[ng, :, hi] + prec[ng, :, hi])
+    def pcopy(i, w):
+        part = pl.ds(0, 2 * w)
+        return pltpu.make_async_remote_copy(pown.at[i, :, part], prec.at[i, :, part],
+                                            c_sent.at[0 if w == half else (5 if w == 256 else 6)], c_p.at[i], partner, MESH)
+
+    def act(i, at, w):
+        took(prec.at[i, :, pl.ds(0, 2 * w)], c_p.at[i])
+        g = pown[i, :, :w] + prec[i, :, :w]
+        u = pown[i, :, w:2 * w] + prec[i, :, w:2 * w]
+        oa[:, pl.ds(pl.multiple_of(ko + at, 128), w)] = (g / (1.0 + jnp.exp(-g)) * u).astype(BF16)
+
+    def product(i, at, w):
+        slot, part = lax.rem(i, slots), pl.ds(0, 2 * w)
+        took(ring.at[slot, :, part], s_w.at[slot])
+        pown[i, :, part] = _dot(nv[...], ring[slot, :, part])
+        pcopy(i, w).start()
 
     def gu_step(j, _):
-        took(ring.at[lax.rem(j, slots)], s_w.at[lax.rem(j, slots)])
-        pown[j] = _dot(nv[...], ring[lax.rem(j, slots)])
-        pcopy(j).start()
-
-        @pl.when(j + slots < ng)
-        def _():
-            start(gu(j + slots), 0)
-
-        @pl.when(j + slots == ng)
-        def _():
-            loop(0, nl, lambda e: start(gl(e), 0))
+        product(*wide(j))
+
+        @pl.when(j < nm)
+        def _():
+            start(gu(*mid(j)), 0)
+
+        @pl.when(j == nm)
+        def _():
+            start(gu(*last), 0)
 
         @pl.when(j > 1)
         def _():
-            act(j - 2)
+            act(*wide(j - 2))
         return 0
 
-    def gl_step(e, _):
-        part = pl.ds(pl.multiple_of(e * 256, 128), 256)
-        took(ring.at[ng % slots, :, part], s_w.at[slots + e])
-        pown[ng, :, part] = _dot(nv[...], ring[ng % slots, :, part])
-        lcopy(e).start()
+    def mid_step(m, _):
+        product(*mid(m))
+
+        @pl.when(m < 2)
+        def _():
+            act(*wide(ng - 2 + m))
         return 0
 
     lax.fori_loop(0, ng, gu_step, 0)
-    lax.fori_loop(0, nl, gl_step, 0)
+    lax.fori_loop(0, nm, mid_step, 0)
+    product(*last)
     loop(0, nq, lambda j: start(qk(j), 1))
 
     blk = [pl.ds(pl.multiple_of(fx[k] * rows, rows), rows) for k in range(4)]
@@ -163,14 +161,13 @@
         for k in (3, 1, 2):
             ycopy(c, k).start()
 
-    act(ng - 2)
+    loop(0, nm - 2, lambda m: act(*mid(m)))
     ins[3].wait()
     took(wdv.at[0], s_dn.at[0])
-    kk = ko + (ng - 1) * half
+    kk = ko + ng * half + (nm - 2) * 256
     ysend[0] = _dot(oa[:, :kk], wdv[0, :kk])
-    act(ng - 1)
-    took(prec.at[ng], c_p.at[ng])
-    loop(0, nl, last_act)
+    loop(nm - 2, nm, lambda m: act(*mid(m)))
+    act(*last)
     ysend[0] = ysend[0] + _dot(oa[:, kk:], wdv[0, kk:])
     scatter(0)
 
@@ -212,7 +209,9 @@
         scopy(k, t).start()
     loop(ny // 2, ny, spread)
     qown[...] = jnp.zeros_like(qown)
-    took(pown, c_sent.at[0])
+    took(pown.at[pl.ds(0, ng)], c_sent.at[0])
+    took(pown.at[pl.ds(0, nm), :, pl.ds(0, 512)], c_sent.at[5])
+    took(pown.at[0, :, pl.ds(0, 256)], c_sent.at[6])
     took(ysend.at[:, pl.ds(0, 3 * rows)], c_sent.at[1])
     took(ss2.at[pl.ds(0, 7)], c_sent.at[4])
     took(ss2.at[pl.ds(0, 7)], c_s2.at[0])
@@ -244,7 +243,7 @@
                     wait(qk(j))
 
             for j in js:
-                qown[j] = qown[j] + _dot(nv[:, ks], ring[lax.rem(j + ng + 1, slots), ks])
+                qown[j] = qown[j] + _dot(nv[:, ks], ring[lax.rem(j + ng + nm + 1, slots), ks])
 
             @pl.when(p == 1)
             def _():
@@ -287,9 +286,9 @@
     def body(x, g1, g2, w_gate, w_up, w_down, o, w_o, w_qkv):
         t, d = x.shape
         kd, ko, q = w_down.shape[0], w_o.shape[0], w_qkv.shape[1]
-        slots, half, nl, cw, qw = 6, 384, 3, 256, 768
-        ng, ny, nq, rows = kd // half - 1, d // cw, q // qw, t // 4
-        cfg = (d, kd, ko, slots, half, ng, nl, cw, ny, qw, nq, rows)
+        slots, half, nm, cw, qw = 6, 384, 4, 256, 768
+        ng, ny, nq, rows = (kd - nm * 256) // half, d // cw, q // qw, t // 4
+        cfg = (d, kd, ko, slots, half, ng, nm, cw, ny, qw, nq, rows)
         dma = pltpu.SemaphoreType.DMA
         any_ = pl.BlockSpec(memory_space=pl.ANY)
         vmem = pl.BlockSpec(memory_space=pltpu.VMEM)
@@ -309,14 +308,14 @@
                 pltpu.VMEM((t, d), BF16),
                 pltpu.VMEM((2, t, 128), F32),
                 pltpu.VMEM((8, 1, 128), F32),
-                pltpu.VMEM((ng + 1, t, 2 * half), F32),
-                pltpu.VMEM((ng + 1, t, 2 * half), F32),
+                pltpu.VMEM((ng + nm + 1, t, 2 * half), F32),
+                pltpu.VMEM((ng + nm + 1, t, 2 * half), F32),
                 pltpu.VMEM((ny, t, cw), F32),
                 pltpu.VMEM((3, ny, rows, cw), F32),
                 pltpu.VMEM((nq, t, qw), F32),
                 pltpu.VMEM((nq, t, qw), F32),
-                dma((3,)), dma((slots + nl,)), dma((ny,)),
-                dma((2,)), dma((ng + 1,)), dma((ny,)), dma((2,)), dma((1,)), dma(((nq + 1) // 2,)), dma((5,)),
+                dma((3,)), dma((slots,)), dma((ny,)),
+                dma((2,)), dma((ng + nm + 1,)), dma((ny,)), dma((2,)), dma((1,)), dma(((nq + 1) // 2,)), dma((7,)),
             ],
             compiler_params=pltpu.CompilerParams(collective_id=0, has_side_effects=True,
                                                  vmem_limit_bytes=60_000_000),

time: 36.6 us -> 36.4 us (level)
  no operation moved by 1% of the time
where the time goes in v5:
time: 36.4 us; the launch traced here: 36.3 us
  Pallas kernels  35.6 us (98%)
  between operations  0.64 us (2%)
    pallas_call x1, Pallas kernels, body(): pl.pallas_call(functools.partial(_kernel, cfg), out_shape=mids, in_specs=...  34.7 us
    pallas_call x1, Pallas kernels, body(): pl.pallas_call(_store, out_shape=outs, in_specs=[vmem, vmem], out_specs=(...  0.91 us

profile of v5, /device:TPU:0, one launch (start us, length us, event | category | flops | bytes accessed | tf_op | source)
XLA Modules:
  0.0 36.3 jit_solution(15530445376240136388)
XLA Ops:
  0.6 34.7 %block.1 = (bf16[64,2560]{1,0:T(8,128)(2,1)S(1)}, bf16[64,3840]{1,0:T(8,128)(2,1)S(1)}) custom-call(bf16[64,2560]{1,0:T(8,128)(2,1)} %x_hbm.1, f32[20,128]{1,0:T(8,128)} %bitcast.2, f32[20,128]{1,0:T(8,128)} %bitcast.3, bf16[2560,3456]{1,0:T(8,128)(2,1)} %wg_hbm.1, bf16[2560,3456]{1,0:T(8,128)(2,1)} %wu_hbm.1, bf16[3456,2560]{1,0:T(8,128)(2,1)} %wd_hbm.1, ...), custom_call_target="tpu_custom_call" | custom-call | tf_op jit(solution)/shard_map/block/pallas_call | solution.py:297
  35.4 0.9 %store.1 = (bf16[64,2560]{1,0:T(8,128)(2,1)}, bf16[64,3840]{1,0:T(8,128)(2,1)}) custom-call(bf16[64,2560]{1,0:T(8,128)(2,1)S(1)} %get-tuple-element.4.x_ref, bf16[64,3840]{1,0:T(8,128)(2,1)S(1)} %get-tuple-element.5.q_ref), custom_call_target="tpu_custom_call" | custom-call | tf_op jit(solution)/shard_map/store/pallas_call | solution.py:324

commit v6 on v5

--- a/solution.py
+++ b/solution.py
@@ -47,8 +47,8 @@
 
     def dn(c):
         cols = pl.ds(pl.multiple_of(c * cw, 128), cw)
-        return [pltpu.make_async_copy(wo_hbm.at[:, cols], wdv.at[c, pl.ds(0, ko)], s_dn.at[c]),
-                pltpu.make_async_copy(wd_hbm.at[:, cols], wdv.at[c, pl.ds(ko, kd)], s_dn.at[c])]
+        return [pltpu.make_async_copy(wo_hbm.at[:, cols], wdv.at[c, pl.ds(0, ko)], s_dn.at[lax.rem(c, ny // 2)]),
+                pltpu.make_async_copy(wd_hbm.at[:, cols], wdv.at[c, pl.ds(ko, kd)], s_dn.at[lax.rem(c, ny // 2)])]
 
     def qk(j):
         slot, cols = lax.rem(j + ng + nm + 1, slots), pl.ds(pl.multiple_of(j * qw, 128), qw)
@@ -71,7 +71,7 @@
     ins = small()
     start(ins, 0)
     loop(0, ng, lambda j: start(gu(*wide(j)), 0))
-    loop(0, ny, lambda c: start(dn(c), 1))
+    loop(0, ny // 2, lambda c: start(dn(c), 1))
 
     barrier = pltpu.get_barrier_semaphore()
     for k in range(4):
@@ -95,8 +95,7 @@
 
     def pcopy(i, w):
         part = pl.ds(0, 2 * w)
-        return pltpu.make_async_remote_copy(pown.at[i, :, part], prec.at[i, :, part],
-                                            c_sent.at[0 if w == half else (5 if w == 256 else 6)], c_p.at[i], partner, MESH)
+        return pltpu.make_async_remote_copy(pown.at[i, :, part], prec.at[i, :, part], c_sent.at[0], c_p.at[i], partner, MESH)
 
     def act(i, at, w):
         took(prec.at[i, :, pl.ds(0, 2 * w)], c_p.at[i])
@@ -137,7 +136,6 @@
     lax.fori_loop(0, ng, gu_step, 0)
     lax.fori_loop(0, nm, mid_step, 0)
     product(*last)
-    loop(0, nq, lambda j: start(qk(j), 1))
 
     blk = [pl.ds(pl.multiple_of(fx[k] * rows, rows), rows) for k in range(4)]
     mine = blk[0]
@@ -146,7 +144,7 @@
         return pl.ds(pl.multiple_of(c * cw, 128), cw)
 
     def ycopy(c, k):
-        return pltpu.make_async_remote_copy(ysend.at[c, blk[k]], yrec.at[k - 1, c], c_sent.at[1], c_y.at[c],
+        return pltpu.make_async_remote_copy(ysend.at[c, blk[k]], yrec.at[k - 1, c], c_sent.at[1], c_y.at[lax.div(c, ny // 2) * (c - ny // 2 + 1)],
                                             (fx[k], h), MESH)
 
     def xcopy(c, k):
@@ -164,6 +162,7 @@
     loop(0, nm - 2, lambda m: act(*mid(m)))
     ins[3].wait()
     took(wdv.at[0], s_dn.at[0])
+    start(dn(ny // 2), 1)
     kk = ko + ng * half + (nm - 2) * 256
     ysend[0] = _dot(oa[:, :kk], wdv[0, :kk])
     loop(nm - 2, nm, lambda m: act(*mid(m)))
@@ -172,7 +171,16 @@
     scatter(0)
 
     def dn_step(c, _):
-        took(wdv.at[c], s_dn.at[c])
+        took(wdv.at[c], s_dn.at[lax.rem(c, ny // 2)])
+
+        @pl.when(c < ny // 2)
+        def _():
+            start(dn(c + ny // 2), 1)
+
+        @pl.when(c == ny // 2 - 1)
+        def _():
+            loop(0, nq, lambda j: start(qk(j), 1))
+
         ysend[c] = _dot(oa[...], wdv[c])
         scatter(c)
         return 0
@@ -180,7 +188,10 @@
     lax.fori_loop(1, ny, dn_step, 0)
 
     def block(c, s):
-        took(yrec.at[:, c], c_y.at[c])
+        @pl.when(c >= ny // 2)
+        def _():
+            took(yrec.at[:, c], c_y.at[c - ny // 2 + 1])
+
         y = (ysend[c, mine] + yrec[0, c]) + (yrec[1, c] + yrec[2, c])
         xn = (xv[mine, chunk(c)].astype(F32) + y).astype(BF16)
         xnv[mine, chunk(c)] = xn
@@ -192,6 +203,7 @@
         xf = xn.astype(F32)
         return s + jnp.sum(xf * xf, axis=-1, keepdims=True)
 
+    took(yrec.at[:, pl.ds(0, ny // 2)], c_y.at[0])
     s = lax.fori_loop(0, ny, block, jnp.zeros((rows, 1), F32))
 
     def diag(n, first):
@@ -209,9 +221,7 @@
         scopy(k, t).start()
     loop(ny // 2, ny, spread)
     qown[...] = jnp.zeros_like(qown)
-    took(pown.at[pl.ds(0, ng)], c_sent.at[0])
-    took(pown.at[pl.ds(0, nm), :, pl.ds(0, 512)], c_sent.at[5])
-    took(pown.at[0, :, pl.ds(0, 256)], c_sent.at[6])
+    took(pown.at[pl.ds(0, kd // half)], c_sent.at[0])
     took(ysend.at[:, pl.ds(0, 3 * rows)], c_sent.at[1])
     took(ss2.at[pl.ds(0, 7)], c_sent.at[4])
     took(ss2.at[pl.ds(0, 7)], c_s2.at[0])
@@ -314,8 +324,8 @@
                 pltpu.VMEM((3, ny, rows, cw), F32),
                 pltpu.VMEM((nq, t, qw), F32),
                 pltpu.VMEM((nq, t, qw), F32),
-                dma((3,)), dma((slots,)), dma((ny,)),
-                dma((2,)), dma((ng + nm + 1,)), dma((ny,)), dma((2,)), dma((1,)), dma(((nq + 1) // 2,)), dma((7,)),
+                dma((3,)), dma((slots,)), dma((ny // 2,)),
+                dma((2,)), dma((ng + nm + 1,)), dma((ny - ny // 2 + 1,)), dma((2,)), dma((1,)), dma(((nq + 1) // 2,)), dma((5,)),
             ],
             compiler_params=pltpu.CompilerParams(collective_id=0, has_side_effects=True,
                                                  vmem_limit_bytes=60_000_000),

time: 36.4 us -> 36.2 us (level)
  no operation moved by 1% of the time
where the time goes in v6:
time: 36.2 us; the launch traced here: 36.1 us
  Pallas kernels  35.5 us (98%)
  between operations  0.64 us (2%)
    pallas_call x1, Pallas kernels, body(): pl.pallas_call(functools.partial(_kernel, cfg), out_shape=mids, in_specs=...  34.6 us
    pallas_call x1, Pallas kernels, body(): pl.pallas_call(_store, out_shape=outs, in_specs=[vmem, vmem], out_specs=(...  0.91 us

profile of v6, /device:TPU:0, one launch (start us, length us, event | category | flops | bytes accessed | tf_op | source)
XLA Modules:
  0.0 36.1 jit_solution(6136863841954277780)
XLA Ops:
  0.6 34.6 %block.1 = (bf16[64,2560]{1,0:T(8,128)(2,1)S(1)}, bf16[64,3840]{1,0:T(8,128)(2,1)S(1)}) custom-call(bf16[64,2560]{1,0:T(8,128)(2,1)} %x_hbm.1, f32[20,128]{1,0:T(8,128)} %bitcast.2, f32[20,128]{1,0:T(8,128)} %bitcast.3, bf16[2560,3456]{1,0:T(8,128)(2,1)} %wg_hbm.1, bf16[2560,3456]{1,0:T(8,128)(2,1)} %wu_hbm.1, bf16[3456,2560]{1,0:T(8,128)(2,1)} %wd_hbm.1, ...), custom_call_target="tpu_custom_call" | custom-call | tf_op jit(solution)/shard_map/block/pallas_call | solution.py:307
  35.2 0.9 %store.1 = (bf16[64,2560]{1,0:T(8,128)(2,1)}, bf16[64,3840]{1,0:T(8,128)(2,1)}) custom-call(bf16[64,2560]{1,0:T(8,128)(2,1)S(1)} %get-tuple-element.4.x_ref, bf16[64,3840]{1,0:T(8,128)(2,1)S(1)} %get-tuple-element.5.q_ref), custom_call_target="tpu_custom_call" | custom-call | tf_op jit(solution)/shard_map/store/pallas_call | solution.py:334

commit v7 on v6

--- a/solution.py
+++ b/solution.py
@@ -286,8 +286,8 @@
 def _store(x_ref, q_ref, xo_hbm, qo_hbm, sem):
     cx = pltpu.make_async_copy(x_ref, xo_hbm, sem.at[0])
     cq = pltpu.make_async_copy(q_ref, qo_hbm, sem.at[1])
+    cq.start()
     cx.start()
-    cq.start()
     cx.wait()
     cq.wait()
 

time: 36.2 us -> 36.2 us (level)
  no operation moved by 1% of the time
where the time goes in v7:
time: 36.2 us; the launch traced here: 36.1 us
  Pallas kernels  35.5 us (98%)
  between operations  0.64 us (2%)
    pallas_call x1, Pallas kernels, body(): pl.pallas_call(functools.partial(_kernel, cfg), out_shape=mids, in_specs=...  34.6 us
    pallas_call x1, Pallas kernels, body(): pl.pallas_call(_store, out_shape=outs, in_specs=[vmem, vmem], out_specs=(...  0.91 us

profile of v7, /device:TPU:0, one launch (start us, length us, event | category | flops | bytes accessed | tf_op | source)
XLA Modules:
  0.0 36.1 jit_solution(10309533698465756201)
XLA Ops:
  0.6 34.6 %block.1 = (bf16[64,2560]{1,0:T(8,128)(2,1)S(1)}, bf16[64,3840]{1,0:T(8,128)(2,1)S(1)}) custom-call(bf16[64,2560]{1,0:T(8,128)(2,1)} %x_hbm.1, f32[20,128]{1,0:T(8,128)} %bitcast.2, f32[20,128]{1,0:T(8,128)} %bitcast.3, bf16[2560,3456]{1,0:T(8,128)(2,1)} %wg_hbm.1, bf16[2560,3456]{1,0:T(8,128)(2,1)} %wu_hbm.1, bf16[3456,2560]{1,0:T(8,128)(2,1)} %wd_hbm.1, ...), custom_call_target="tpu_custom_call" | custom-call | tf_op jit(solution)/shard_map/block/pallas_call | solution.py:307
  35.2 0.9 %store.1 = (bf16[64,2560]{1,0:T(8,128)(2,1)}, bf16[64,3840]{1,0:T(8,128)(2,1)}) custom-call(bf16[64,2560]{1,0:T(8,128)(2,1)S(1)} %get-tuple-element.4.x_ref, bf16[64,3840]{1,0:T(8,128)(2,1)S(1)} %get-tuple-element.5.q_ref), custom_call_target="tpu_custom_call" | custom-call | tf_op jit(solution)/shard_map/store/pallas_call | solution.py:334
